TPU v7x, 8 devices: a whole 2x2x1 slice. The times are simulated.
8 devices in a mesh: tp: 2 (over z, y), ep: 4 (over x, core).
Axes of the slice: x: 2, y: 2, z: 1, core: 2. Of those that a mesh axis runs over, the one named last changes fastest.
Arguments:
- x_norm: bfloat16 [4096, 1024], P(('ep', 'tp'))
- route_idx: int32 [4096, 8], P(('ep', 'tp'))
- route_slot: int32 [4096, 8], P(('ep', 'tp'))
- w_router: bfloat16 [1024, 32], replicated
- b_router: float32 [32], replicated
- w_gate_up: bfloat16 [32, 1024, 1024], P('ep', None, 'tp')
- b_gate_up: float32 [32, 1024], P('ep', 'tp')
- w_down: bfloat16 [32, 512, 1024], P('ep', 'tp')
- b_down: float32 [32, 1024], P('ep')
- d_out: bfloat16 [4096, 1024], P(('ep', 'tp'))
Outputs:
- output 1: bfloat16 [4096, 1024], P(('ep', 'tp'))
- output 2: bfloat16 [4096, 1024], P(('ep', 'tp'))
- output 3: bfloat16 [32, 1024, 1024], P('ep', None, 'tp')
- output 4: float32 [32, 1024], P('ep', 'tp')
- output 5: bfloat16 [32, 512, 1024], P('ep', 'tp')
- output 6: float32 [32, 1024], P('ep')
- output 7: float32 [1024, 32], replicated
- output 8: float32 [32], replicated
All inputs are finite; a program needn't handle non-finite values.
Results may differ from a plain program's by a relative error of at most 0.0122516.
Values are sent between devices in bfloat16 or wider.
A program may use at most 1 GiB of HBM per device.

v0:
```python
import jax
import jax.numpy as jnp
from jax import lax
from jax.sharding import PartitionSpec as P

CLAMP_LIMIT = 7.0
SWIGLU_ALPHA = 1.702


def clamped_swiglu(h_pair):
    gate_val = jnp.minimum(h_pair[..., 0], CLAMP_LIMIT)
    up_val = jnp.clip(h_pair[..., 1], -CLAMP_LIMIT, CLAMP_LIMIT)
    return gate_val * jax.nn.sigmoid(SWIGLU_ALPHA * gate_val) * (up_val + 1.0)


def solution(mesh):
    tp_count = mesh.shape['tp']
    ep_count = mesh.shape['ep']
    tok_spec = P(('ep', 'tp'), None)

    def device_fn(x_loc, idx_loc, slot_loc, w_router, b_router, w_gate_up, b_gate_up, w_down, b_down, dy_loc):
        tok_count, model_dim = x_loc.shape
        top_k = idx_loc.shape[1]
        n_experts = w_router.shape[1]
        local_experts = w_gate_up.shape[0]
        shard_width = w_gate_up.shape[2] // 2
        capacity = 2 * tok_count * top_k // n_experts
        buf_rows = n_experts * capacity
        tp_index = lax.axis_index('tp')

        def dispatch(buf_in):
            gathered = lax.all_gather(buf_in.reshape(n_experts, capacity, model_dim), 'tp', axis=0)
            moved = lax.all_to_all(gathered, 'ep', 1, 1, tiled=True)
            return moved.reshape(tp_count, ep_count, local_experts, capacity, model_dim)

        def collect(part_in):
            back = lax.all_to_all(part_in.reshape(tp_count, n_experts, capacity, model_dim), 'ep', 1, 1, tiled=True)
            per_shard = lax.all_to_all(back, 'tp', 0, 0, tiled=True)
            return jnp.sum(per_shard, axis=0, dtype=jnp.float32).astype(jnp.bfloat16).reshape(buf_rows, model_dim)

        logits = jnp.dot(x_loc, w_router, preferred_element_type=jnp.float32) + b_router[None, :]
        expert_hot = idx_loc[:, :, None] == jnp.arange(n_experts)[None, None, :]
        picked = jnp.sum(jnp.where(expert_hot, logits[:, None, :], 0.0), axis=2)
        gate_w = jax.nn.softmax(picked, axis=1)
        flat_pos = jnp.where(slot_loc >= 0, idx_loc * capacity + slot_loc, -1)
        pick_mat = (flat_pos[:, :, None] == jnp.arange(buf_rows)[None, None, :]).astype(jnp.bfloat16)
        send_mat = jnp.max(pick_mat, axis=1)
        send_rows = jnp.einsum('tp,td->pd', send_mat, x_loc, preferred_element_type=jnp.float32).astype(jnp.bfloat16)

        recv_rows = dispatch(send_rows)
        hidden_pre = jnp.einsum('sgecd,edf->sgecf', recv_rows, w_gate_up, preferred_element_type=jnp.float32) + b_gate_up[None, None, :, None, :]
        h_pair = hidden_pre.reshape(hidden_pre.shape[:-1] + (shard_width, 2))
        act_f32, act_pull = jax.vjp(clamped_swiglu, h_pair)
        act_val = act_f32.astype(jnp.bfloat16)
        bias_on = (tp_index == 0).astype(jnp.float32)
        part_out = jnp.einsum('sgecf,efd->sgecd', act_val, w_down, preferred_element_type=jnp.float32)
        part_out = (part_out + bias_on * b_down[None, None, :, None, :]).astype(jnp.bfloat16)
        y_buf = collect(part_out)
        y_pick = jnp.einsum('tkp,pd->tkd', pick_mat, y_buf, preferred_element_type=jnp.float32)
        moe_out = jnp.sum(gate_w[:, :, None] * y_pick, axis=1).astype(jnp.bfloat16)

        d_out32 = dy_loc.astype(jnp.float32)
        d_gate = jnp.sum(y_pick * d_out32[:, None, :], axis=2)
        d_picked = gate_w * (d_gate - jnp.sum(gate_w * d_gate, axis=1, keepdims=True))
        d_logits = jnp.sum(jnp.where(expert_hot, d_picked[:, :, None], 0.0), axis=1)
        d_copy = (gate_w[:, :, None] * d_out32[:, None, :]).astype(jnp.bfloat16)
        d_send = jnp.einsum('tkp,tkd->pd', pick_mat, d_copy, preferred_element_type=jnp.float32).astype(jnp.bfloat16)
        d_recv = dispatch(d_send)
        grad_w_down = jnp.einsum('sgecf,sgecd->efd', act_val, d_recv, preferred_element_type=jnp.float32).astype(jnp.bfloat16)
        grad_b_down = jnp.sum(d_recv, axis=(0, 1, 3), dtype=jnp.float32)
        d_act = jnp.einsum('sgecd,efd->sgecf', d_recv, w_down, preferred_element_type=jnp.float32)
        d_pair = act_pull(d_act)[0]
        d_hidden = d_pair.reshape(hidden_pre.shape)
        grad_b_gate_up = jnp.sum(d_hidden, axis=(0, 1, 3))
        d_hidden_b = d_hidden.astype(jnp.bfloat16)
        grad_w_gate_up = jnp.einsum('sgecd,sgecf->edf', recv_rows, d_hidden_b, preferred_element_type=jnp.float32).astype(jnp.bfloat16)
        d_rows_part = jnp.einsum('sgecf,edf->sgecd', d_hidden_b, w_gate_up, preferred_element_type=jnp.float32).astype(jnp.bfloat16)
        d_rows = collect(d_rows_part)
        d_logits_b = d_logits.astype(jnp.bfloat16)
        d_x = jnp.einsum('tp,pd->td', send_mat, d_rows, preferred_element_type=jnp.float32) + jnp.einsum('te,de->td', d_logits_b, w_router, preferred_element_type=jnp.float32)
        grad_w_router = lax.psum(jnp.einsum('td,te->de', x_loc, d_logits_b, preferred_element_type=jnp.float32), ('tp', 'ep'))
        grad_b_router = lax.psum(jnp.sum(d_logits, axis=0), ('tp', 'ep'))
        return (moe_out, d_x.astype(jnp.bfloat16), grad_w_gate_up, grad_b_gate_up, grad_w_down, grad_b_down, grad_w_router, grad_b_router)

    in_specs = (tok_spec, tok_spec, tok_spec, P(None, None), P(None), P('ep', None, 'tp'), P('ep', 'tp'), P('ep', 'tp', None), P('ep', None), tok_spec)
    out_specs = (tok_spec, tok_spec, P('ep', None, 'tp'), P('ep', 'tp'), P('ep', 'tp', None), P('ep', None), P(None, None), P(None))
    return jax.shard_map(device_fn, mesh=mesh, in_specs=in_specs, out_specs=out_specs, check_vma=False)
```

profile of v0, /device:TPU:0, one launch (start us, length us, event | category | flops | bytes accessed | tf_op | source)
XLA Modules:
  0.0 2911.5 jit_solution(7089927528477895099)
XLA Ops:
  8.0 45.5 %fusion.3 = bf16[512,8192]{0,1:T(8,128)(2,1)} fusion(s32[512,8]{0,1:T(8,128)S(1)} %add_select_fusion), kind=kLoop, calls=%fused_computation.4 | loop fusion | flops 96468992 | bytes 8404992 | tf_op jit(solution)/shard_map/reduce_max | solution.py:47
  72.6 72.7 %bitcast_convert_fusion = bf16[8192,1024]{1,0:T(8,128)(2,1)} fusion(s32[512,8]{0,1:T(8,128)S(1)} %add_select_fusion, bf16[512,8,1024]{2,0,1:T(8,128)(2,1)S(1)} %multiply_convert_fusion.5), kind=kOutput, calls=%fused_computation.16 | convolution fusion | flops 68761419776 | bytes 25182208 | tf_op jit(solution)/shard_map/tkp,tkd->pd/dot_general | solution.py:67
  145.3 312.6 %all-gather.3.cloned.1.call-done = bf16[2,32,256,1024]{3,2,1,0:T(8,128)(2,1)} async-done(((bf16[1,32,256,1024]{3,2,1,0:T(8,128)(2,1)}), bf16[2,32,256,1024]{3,2,1,0:T(8,128)(2,1)}) %all-gather.3.cloned.1.call-update) | async-done | bytes 33554448 | tf_op jit(solution)/shard_map/all_gather | solution.py:32
  457.9 22.6 copy.102
  490.2 354.7 %all-gather.5.cloned.1.call-done = bf16[2,32,256,1024]{3,2,1,0:T(8,128)(2,1)} async-done(((bf16[1,32,256,1024]{3,2,1,0:T(8,128)(2,1)}), bf16[2,32,256,1024]{3,2,1,0:T(8,128)(2,1)}) %all-gather.5.cloned.1.call-update) | async-done | bytes 33554448 | tf_op jit(solution)/shard_map/all_gather | solution.py:32
  845.0 22.6 copy.113
  878.0 31.2 %add_bitcast_fusion = f32[2,4,8,256,512]{4,3,1,0,2:T(8,128)} fusion(f32[8,512]{1,0:T(8,128)S(1)} %copy-done.21, bf16[2,4,8,256,1024]{4,3,0,2,1:T(8,128)(2,1)} %bitcast.2, bf16[8,1024,512]{2,1,0:T(8,128)(2,1)} %param.15), kind=kOutput, calls=%fused_computation.21 | convolution fusion | flops 17188257792 | bytes 75513856 | tf_op jit(solution)/shard_map/sgecd,edf->sgecf/dot_general | solution.py:51
  909.2 39.7 %copy.105 = f32[2,4,8,256,512]{3,2,4,1,0:T(8,128)} copy(f32[2,4,8,256,512]{4,3,1,0,2:T(8,128)} %add_bitcast_fusion) | data formatting | bytes 67108864 | tf_op jit(solution)/shard_map/add | solution.py:51
  970.7 269.1 %all-to-all-done.3 = bf16[2,32,256,1024]{3,2,0,1:T(8,128)(2,1)} async-done(((bf16[2,32,256,1024]{3,2,0,1:T(8,128)(2,1)}), bf16[2,32,256,1024]{3,2,0,1:T(8,128)(2,1)}, u32[]{:S(2)}, u32[]{:S(2)}) %all-to-all-start.3) | async-done | bytes 33554464 | tf_op jit(solution)/shard_map/all_to_all | solution.py:33
  1239.8 45.7 %fusion.22 = (f32[2,4,8,256,256,1]{3,4,1,0,2,5:T(8,128)}, f32[2,4,8,256,256,1]{3,4,1,0,2,5:T(8,128)}, bf16[2,4,8,256,256]{3,4,1,0,2:T(8,128)(2,1)}) fusion(f32[2,4,8,256,256,1]{3,2,5,4,1,0:T(8,128)} %get-tuple-element.50, f32[2,4,8,256,256,1]{3,2,5,4,1,0:T(8,128)} %get-tuple-element.49, bf16[8,256,1024]{2,1,0:T(8,128)(2,1)} %param.17, ...), kind=kOutput, calls=%fused_computation.32 | convolution fusion | flops 8736735232 | bytes 113246208 | tf_op jit(solution)/shard_map/sgecd,efd->sgecf/dot_general | solution.py:71
  1303.6 22.7 copy.109
  1326.3 22.7 copy.110
  1382.5 29.0 convert_bitcast_fusion
  1411.5 22.7 copy.118
  1434.2 22.7 copy.119
  1456.8 264.7 %all-to-all-done.1 = bf16[2,32,256,1024]{3,2,0,1:T(8,128)(2,1)} async-done(((bf16[2,32,256,1024]{3,2,0,1:T(8,128)(2,1)}), bf16[2,32,256,1024]{3,2,0,1:T(8,128)(2,1)}, u32[]{:S(2)}, u32[]{:S(2)}) %all-to-all-start.1) | async-done | bytes 33554464 | tf_op jit(solution)/shard_map/all_to_all | solution.py:37
  1731.4 22.7 copy.111
  1754.1 339.8 %all-to-all-done.4 = bf16[2,32,256,1024]{3,2,0,1:T(8,128)(2,1)} async-done(((bf16[2,32,256,1024]{3,2,0,1:T(8,128)(2,1)}), bf16[2,32,256,1024]{3,2,0,1:T(8,128)(2,1)}, u32[]{:S(2)}, u32[]{:S(2)}) %all-to-all-start.4) | async-done | bytes 33554464 | tf_op jit(solution)/shard_map/all_to_all | solution.py:37
  2119.5 22.6 copy.120
  2142.1 326.4 %all-to-all-done.2 = bf16[2,32,256,1024]{3,2,1,0:T(8,128)(2,1)} async-done(((bf16[2,32,256,1024]{3,2,1,0:T(8,128)(2,1)}), bf16[2,32,256,1024]{3,2,1,0:T(8,128)(2,1)}, u32[]{:S(2)}, u32[]{:S(2)}) %all-to-all-start.2) | async-done | bytes 33554464 | tf_op jit(solution)/shard_map/all_to_all | solution.py:38
  2499.9 36.7 %bitcast_convert_fusion.1 = bf16[8,1024,512]{2,1,0:T(8,128)(2,1)} fusion(bf16[2,4,8,256,512]{3,2,4,1,0:T(8,128)(2,1)} %bitcast.123, bf16[2,4,8,256,1024]{4,3,0,2,1:T(8,128)(2,1)} %bitcast.2), kind=kOutput, calls=%fused_computation.30 | convolution fusion | flops 17184063488 | bytes 58720256 | tf_op jit(solution)/shard_map/sgecd,sgecf->edf/dot_general | solution.py:76
  2557.5 79.0 %multiply_reduce_fusion = (f32[512,8]{0,1:T(8,128)S(1)}, bf16[512,1024]{1,0:T(8,128)(2,1)}) fusion(f32[512,1024]{1,0:T(8,128)S(1)} %copy-done.2, f32[512,8]{0,1:T(8,128)S(1)} %copy-done.12, bf16[8192,1024,1]{1,0,2:T(8,128)(2,1)} %bitcast.126, s32[512,8]{0,1:T(8,128)S(1)} %copy-done.10), kind=kOutput, calls=%fused_computation.47 | convolution fusion | flops 68769284096 | bytes 19972096 | tf_op jit(solution)/shard_map/tkp,pd->tkd/dot_general | solution.py:59
  2638.3 205.8 %all-to-all-done.5 = bf16[2,32,256,1024]{3,2,1,0:T(8,128)(2,1)} async-done(((bf16[2,32,256,1024]{3,2,1,0:T(8,128)(2,1)}), bf16[2,32,256,1024]{3,2,1,0:T(8,128)(2,1)}, u32[]{:S(2)}, u32[]{:S(2)}) %all-to-all-start.5) | async-done | bytes 33554464 | tf_op jit(solution)/shard_map/all_to_all | solution.py:38
  2880.8 22.2 psum.15
  (86 shorter events, 241.1 us)
Async XLA Ops:
  7.2 46.4 %copy-start = (bf16[512,1024]{1,0:T(8,128)(2,1)S(1)}, bf16[512,1024]{1,0:T(8,128)(2,1)}, u32[]{:S(2)}) copy-start(bf16[512,1024]{1,0:T(8,128)(2,1)} %param.10) | copy-start | bytes 3145732
  7.2 450.7 %all-gather.3.cloned.1.call-start = ((), (), s32[]{:S(2)}) async-start(), calls=%async_computation.6 | async-start | bytes 50331648 | tf_op jit(solution)/shard_map/all_gather | solution.py:32
  8.0 64.5 %copy-start.9 = (s32[512,8]{0,1:T(8,128)}, s32[512,8]{0,1:T(8,128)S(1)}, u32[]{:S(2)}) copy-start(s32[512,8]{0,1:T(8,128)S(1)} %add_select_fusion) | copy-start | bytes 49156
  69.4 775.6 %all-gather.5.cloned.1.call-start = ((), (), s32[]{:S(2)}) async-start(), calls=%async_computation.7 | async-start | bytes 50331648 | tf_op jit(solution)/shard_map/all_gather | solution.py:32
  71.0 74.3 %copy-start.1 = (f32[512,1024]{1,0:T(8,128)}, f32[512,1024]{1,0:T(8,128)S(1)}, u32[]{:S(2)}) copy-start(f32[512,1024]{1,0:T(8,128)S(1)} %convert_element_type.69) | copy-start | bytes 6291460
  71.5 73.8 %copy-start.3 = (f32[512,8]{0,1:T(8,128)}, f32[512,8]{0,1:T(8,128)S(1)}, u32[]{:S(2)}) copy-start(f32[512,8]{0,1:T(8,128)S(1)} %select_reduce_fusion.2) | copy-start | bytes 49156
  71.5 73.8 %copy-start.13 = (f32[512]{0:T(512)}, f32[512]{0:T(512)S(1)}, u32[]{:S(2)}) copy-start(f32[512]{0:T(512)S(1)} %reduce_max.18) | copy-start | bytes 6148
  71.6 73.7 %copy-start.15 = (f32[512]{0:T(512)}, f32[512]{0:T(512)S(1)}, u32[]{:S(2)}) copy-start(f32[512]{0:T(512)S(1)} %fusion.51) | copy-start | bytes 6148
  71.6 73.7 %copy-start.11 = (f32[512,8]{0,1:T(8,128)}, f32[512,8]{0,1:T(8,128)S(1)}, u32[]{:S(2)}) copy-start(f32[512,8]{0,1:T(8,128)S(1)} %fusion.50) | copy-start | bytes 49156
  480.5 387.1 %all-to-all-start = ((bf16[2,32,256,1024]{3,2,0,1:T(8,128)(2,1)}), bf16[2,32,256,1024]{3,2,0,1:T(8,128)(2,1)}, u32[]{:S(2)}, u32[]{:S(2)}) async-start(bf16[2,32,256,1024]{3,2,0,1:T(8,128)(2,1)} %copy.102), calls=%async_computation | async-start | bytes 67108864 | tf_op jit(solution)/shard_map/all_to_all | solution.py:33
  867.6 372.2 %all-to-all-start.3 = ((bf16[2,32,256,1024]{3,2,0,1:T(8,128)(2,1)}), bf16[2,32,256,1024]{3,2,0,1:T(8,128)(2,1)}, u32[]{:S(2)}, u32[]{:S(2)}) async-start(bf16[2,32,256,1024]{3,2,0,1:T(8,128)(2,1)} %copy.113), calls=%async_computation.3 | async-start | bytes 67108864 | tf_op jit(solution)/shard_map/all_to_all | solution.py:33
  1239.8 45.7 %copy-start.18 = (f32[8,1024]{1,0:T(8,128)S(1)}, f32[8,1024]{1,0:T(8,128)}, u32[]{:S(2)}) copy-start(f32[8,1024]{1,0:T(8,128)} %broadcast_multiply_fusion) | copy-start | bytes 98308
  1239.8 45.7 %copy-start.20 = (bf16[8,256,1024]{2,1,0:T(8,128)(2,1)S(1)}, bf16[8,256,1024]{2,1,0:T(8,128)(2,1)}, u32[]{:S(2)}) copy-start(bf16[8,256,1024]{2,1,0:T(8,128)(2,1)} %param.17) | copy-start | bytes 12582916
  1349.0 372.6 %all-to-all-start.1 = ((bf16[2,32,256,1024]{3,2,0,1:T(8,128)(2,1)}), bf16[2,32,256,1024]{3,2,0,1:T(8,128)(2,1)}, u32[]{:S(2)}, u32[]{:S(2)}) async-start(bf16[2,32,256,1024]{3,2,0,1:T(8,128)(2,1)} %copy.110), calls=%async_computation.1 | async-start | bytes 67108864 | tf_op jit(solution)/shard_map/all_to_all | solution.py:37
  1721.5 372.3 %all-to-all-start.4 = ((bf16[2,32,256,1024]{3,2,0,1:T(8,128)(2,1)}), bf16[2,32,256,1024]{3,2,0,1:T(8,128)(2,1)}, u32[]{:S(2)}, u32[]{:S(2)}) async-start(bf16[2,32,256,1024]{3,2,0,1:T(8,128)(2,1)} %copy.119), calls=%async_computation.4 | async-start | bytes 67108864 | tf_op jit(solution)/shard_map/all_to_all | solution.py:37
  2093.8 374.7 %all-to-all-start.2 = ((bf16[2,32,256,1024]{3,2,1,0:T(8,128)(2,1)}), bf16[2,32,256,1024]{3,2,1,0:T(8,128)(2,1)}, u32[]{:S(2)}, u32[]{:S(2)}) async-start(bf16[2,32,256,1024]{3,2,1,0:T(8,128)(2,1)} %copy.111), calls=%async_computation.2 | async-start | bytes 67108864 | tf_op jit(solution)/shard_map/all_to_all | solution.py:38
  2468.6 375.5 %all-to-all-start.5 = ((bf16[2,32,256,1024]{3,2,1,0:T(8,128)(2,1)}), bf16[2,32,256,1024]{3,2,1,0:T(8,128)(2,1)}, u32[]{:S(2)}, u32[]{:S(2)}) async-start(bf16[2,32,256,1024]{3,2,1,0:T(8,128)(2,1)} %copy.120), calls=%async_computation.5 | async-start | bytes 67108864 | tf_op jit(solution)/shard_map/all_to_all | solution.py:38
  2481.5 421.5 %all-reduce.4.cloned.1.call-start = ((), (), s32[]{:S(2)}) async-start(), calls=%async_computation.8 | async-start | bytes 262144 | tf_op jit(solution)/shard_map/psum | solution.py:81
  2536.6 20.9 copy-start.12
  2557.5 79.1 %copy-start.4 = (f32[512,8]{0,1:T(8,128)S(1)}, f32[512,8]{0,1:T(8,128)}, u32[]{:S(2)}) copy-start(f32[512,8]{0,1:T(8,128)} %copy-done.3) | copy-start | bytes 49156
  2557.5 79.1 %copy-start.14 = (f32[512]{0:T(512)S(1)}, f32[512]{0:T(512)}, u32[]{:S(2)}) copy-start(f32[512]{0:T(512)} %copy-done.13) | copy-start | bytes 6148
  2557.5 79.1 %copy-start.16 = (f32[512]{0:T(512)S(1)}, f32[512]{0:T(512)}, u32[]{:S(2)}) copy-start(f32[512]{0:T(512)} %copy-done.15) | copy-start | bytes 6148
  2557.5 79.1 %copy-start.8 = (s32[512,8]{0,1:T(8,128)S(1)}, s32[512,8]{0,1:T(8,128)}, u32[]{:S(2)}) copy-start(s32[512,8]{0,1:T(8,128)} %param.11) | copy-start | bytes 49156
  2557.5 80.3 %copy-start.6 = (bf16[1024,32]{0,1:T(8,128)(2,1)S(1)}, bf16[1024,32]{0,1:T(8,128)(2,1)}, u32[]{:S(2)}) copy-start(bf16[1024,32]{0,1:T(8,128)(2,1)} %param.13) | copy-start | bytes 196612
  (7 other events, 67.0 us)
Sparse Core Ops, SparseCore 0:
  69.5 388.3 all-gather.2
  459.4 385.4 all-gather.4
  2637.9 43.0 all-reduce.3
where the time goes:
time: 2920 us; the launch traced here: 2910 us
  waiting for transfers between devices  2070 us (71%)
  matrix products  364 us (12%)
  local copies, waits for them, and re-layouts  256 us (9%)
  other arithmetic  116 us (4%)
  starting transfers between devices  65.4 us (2%)
    all_gather x2, waiting for transfers between devices, dispatch(): lax.all_gather(buf_in.reshape(n_experts, capacity, model_dim), 'tp', axis=0)  667 us
    all_to_all x2, waiting for transfers between devices, collect(): lax.all_to_all(part_in.reshape(tp_count, n_experts, capacity, model_dim),...  604 us
    all_to_all x2, waiting for transfers between devices, collect(): per_shard = lax.all_to_all(back, 'tp', 0, 0, tiled=True)  532 us
    all_to_all x2, waiting for transfers between devices, dispatch(): moved = lax.all_to_all(gathered, 'ep', 1, 1, tiled=True)  269 us
    dot_general x1, matrix products, device_fn(): jnp.einsum('tkp,pd->tkd', pick_mat, y_buf, preferred_element_type=jnp.flo...  79 us
    dot_general x1, matrix products, device_fn(): jnp.einsum('tkp,tkd->pd', pick_mat, d_copy, preferred_element_type=jnp.fl...  72.7 us
  transfers between devices with their start and end apart: 9, of which 7 were waited for; matrix products, arithmetic and copies ran while one was open for 19% of the time, Pallas kernels for 0%

commit v1 on v0

v1 whole, which is shorter than its diff:
```python
import functools
import jax
import jax.numpy as jnp
from jax import lax
from jax.experimental import pallas as pl
from jax.experimental.pallas import tpu as pltpu
from jax.sharding import PartitionSpec as P

LIMIT = 7.0
ALPHA = 1.702
BF = jnp.bfloat16
F32 = jnp.float32
SIZES = (64, 128, 192, 256)
SEG = 256
KT = 256


def dot(a, b, dims=((1,), (0,))):
    return lax.dot_general(a, b, (dims, ((), ())), preferred_element_type=F32)


def chunk_kernel(cnt_ref, x_ref, d_ref, rk_ref, wv_ref, w1_ref, w1t_ref, w2_ref, w2t_ref, b1_ref, b2_ref,
                 out_ref, dx_ref, dg_ref, gb1_ref, xs_ref, ds_ref, dh_ref, wa_ref,
                 sel, ybuf, dxbuf, acc, off):
    e = pl.program_id(0)
    i = pl.program_id(1)
    n_e = pl.num_programs(0)
    toks = x_ref.shape[1]
    half = w2_ref.shape[1]

    @pl.when(e == 0)
    def _():
        off[i] = 0

    @pl.when(i == 0)
    def _():
        gb1_ref[...] = jnp.zeros_like(gb1_ref)

    count = cnt_ref[e * 2 + i]
    start = pl.multiple_of(off[i], 64)

    def rows(m):
        rk = rk_ref[0, pl.ds(i, 1), :]
        wv = wv_ref[0, pl.ds(i, 1), :]
        pos = lax.broadcasted_iota(jnp.int32, (m, toks), 0).astype(F32)
        hot = jnp.broadcast_to(rk, (m, toks)) == pos
        hot_b = jnp.where(hot, 1.0, 0.0).astype(BF)
        w_row = jnp.sum(jnp.where(hot, jnp.broadcast_to(wv, (m, toks)), 0.0), axis=1, keepdims=True)
        x_rows = dot(hot_b, x_ref[i]).astype(BF)
        d_rows = dot(hot_b, d_ref[i]).astype(BF)
        hid = dot(x_rows, w1_ref[0]) + b1_ref[0]
        gate, up = hid[:, :half], hid[:, half:]
        g = jnp.minimum(gate, LIMIT)
        u1 = jnp.clip(up, -LIMIT, LIMIT) + 1.0
        sg = jax.nn.sigmoid(ALPHA * g)
        gs = g * sg
        act = (gs * u1).astype(BF)
        part = (dot(act, w2_ref[0]) + b2_ref[0]).astype(BF).astype(F32)
        dg_row = jnp.sum(part * d_rows.astype(F32), axis=1, keepdims=True)
        dg_ref[0, pl.ds(i, 1), :] = jnp.sum(jnp.where(hot, dg_row, 0.0), axis=0, keepdims=True)
        ybuf[i, pl.ds(start, m), :] = (w_row * part).astype(BF)
        sel[i, pl.ds(start, m), :] = hot_b
        d_act = w_row * dot(d_rows, w2t_ref[0])
        gate_on = jnp.where(gate < LIMIT, 1.0, jnp.where(gate == LIMIT, 0.5, 0.0))
        up_abs = jnp.abs(up)
        up_on = jnp.where(up_abs < LIMIT, 1.0, jnp.where(up_abs == LIMIT, 0.5, 0.0))
        d_gate = d_act * u1 * (sg * (1.0 + ALPHA * g * (1.0 - sg))) * gate_on
        d_up = d_act * gs * up_on
        d_hid = jnp.concatenate([d_gate, d_up], axis=1)
        gb1_ref[0] += jnp.sum(d_hid, axis=0, keepdims=True)
        d_hid_b = d_hid.astype(BF)
        dxbuf[i, pl.ds(start, m), :] = dot(d_hid_b, w1t_ref[0]).astype(BF)
        xs_ref[0, 0, :m, :] = x_rows
        ds_ref[0, 0, :m, :] = d_rows
        dh_ref[0, 0, :m, :] = d_hid_b
        wa_ref[0, 0, :m, :] = (w_row * act.astype(F32)).astype(BF)
        if m < SEG:
            for ref in (xs_ref, ds_ref, dh_ref, wa_ref):
                ref[0, 0, m:, :] = jnp.zeros((SEG - m, ref.shape[3]), BF)
        off[i] = start + m

    low = 0
    for m in SIZES:
        pl.when((count > low) & (count <= m))(functools.partial(rows, m))
        low = m

    @pl.when(count == 0)
    def _():
        dg_ref[0, pl.ds(i, 1), :] = jnp.zeros((1, toks), F32)
        for ref in (xs_ref, ds_ref, dh_ref, wa_ref):
            ref[...] = jnp.zeros_like(ref)

    @pl.when(e == n_e - 1)
    def _():
        total = off[i]
        fill = pl.multiple_of(total, 64)
        for buf in (sel, ybuf, dxbuf):
            buf[i, pl.ds(fill, KT), :] = jnp.zeros((KT, buf.shape[2]), BF)
        tiles = (total + KT - 1) // KT
        for buf, dst in ((ybuf, out_ref), (dxbuf, dx_ref)):
            acc[...] = jnp.zeros_like(acc)

            def step(k, _):
                at = pl.ds(pl.multiple_of(k * KT, KT), KT)
                acc[...] += dot(sel[i, at, :], buf[i, at, :], ((0,), (0,)))
                return 0

            lax.fori_loop(0, tiles, step, 0)
            dst[i] = acc[...].astype(BF)


def run_chunk(cnt, x2, d2, rk, wv, w1, w1t, w2, w2t, b1, b2):
    n_e, dim, wide = w1.shape
    half = w2.shape[1]
    toks = x2.shape[1]
    whole3 = lambda e, i, c: (0, 0, 0)
    per_e = lambda e, i, c: (e, 0, 0)
    seg = lambda e, i, c: (e, i, 0, 0)
    room = n_e * SEG + KT
    return pl.pallas_call(
        chunk_kernel,
        grid_spec=pltpu.PrefetchScalarGridSpec(
            num_scalar_prefetch=1,
            grid=(n_e, 2),
            in_specs=[
                pl.BlockSpec((2, toks, dim), whole3, pipeline_mode=pl.Buffered(1)),
                pl.BlockSpec((2, toks, dim), whole3, pipeline_mode=pl.Buffered(1)),
                pl.BlockSpec((1, 2, toks), per_e),
                pl.BlockSpec((1, 2, toks), per_e),
                pl.BlockSpec((1, dim, wide), per_e),
                pl.BlockSpec((1, wide, dim), per_e),
                pl.BlockSpec((1, half, dim), per_e),
                pl.BlockSpec((1, dim, half), per_e),
                pl.BlockSpec((1, 1, wide), per_e),
                pl.BlockSpec((1, 1, dim), per_e),
            ],
            out_specs=[
                pl.BlockSpec((2, toks, dim), whole3, pipeline_mode=pl.Buffered(1)),
                pl.BlockSpec((2, toks, dim), whole3, pipeline_mode=pl.Buffered(1)),
                pl.BlockSpec((1, 2, toks), per_e),
                pl.BlockSpec((1, 1, wide), per_e),
                pl.BlockSpec((1, 1, SEG, dim), seg),
                pl.BlockSpec((1, 1, SEG, dim), seg),
                pl.BlockSpec((1, 1, SEG, wide), seg),
                pl.BlockSpec((1, 1, SEG, half), seg),
            ],
            scratch_shapes=[
                pltpu.VMEM((2, room, toks), BF),
                pltpu.VMEM((2, room, dim), BF),
                pltpu.VMEM((2, room, dim), BF),
                pltpu.VMEM((toks, dim), F32),
                pltpu.SMEM((2,), jnp.int32),
            ],
        ),
        out_shape=[
            jax.ShapeDtypeStruct((2, toks, dim), BF),
            jax.ShapeDtypeStruct((2, toks, dim), BF),
            jax.ShapeDtypeStruct((n_e, 2, toks), F32),
            jax.ShapeDtypeStruct((n_e, 1, wide), F32),
            jax.ShapeDtypeStruct((n_e, 2, SEG, dim), BF),
            jax.ShapeDtypeStruct((n_e, 2, SEG, dim), BF),
            jax.ShapeDtypeStruct((n_e, 2, SEG, wide), BF),
            jax.ShapeDtypeStruct((n_e, 2, SEG, half), BF),
        ],
        compiler_params=pltpu.CompilerParams(dimension_semantics=('arbitrary', 'arbitrary'), vmem_limit_bytes=64000 * 1024),
        cost_estimate=pl.CostEstimate(flops=28_000_000_000, bytes_accessed=64_000_000, transcendentals=0),
        name='experts',
    )(cnt, x2, d2, rk, wv, w1, w1t, w2, w2t, b1, b2)


def wgrad_kernel(n_c, *refs):
    xs, ds, dh, wa = (refs[k * n_c:(k + 1) * n_c] for k in range(4))
    mix_ref, gw1_ref, gw2_ref, acc1, acc2 = refs[4 * n_c:]
    lhs = ((0,), (0,))
    for k in range(n_c):
        for i in range(2):
            one = dot(xs[k][0, i], dh[k][0, i], lhs)
            two = dot(wa[k][0, i], ds[k][0, i], lhs)
            if k + i == 0:
                acc1[...] = one
                acc2[...] = two
            else:
                acc1[...] += one
                acc2[...] += two
    gw2_ref[0] = acc2[...].astype(BF)
    gw1_ref[0] = dot(acc1[...].astype(BF), mix_ref[...]).astype(BF)


def run_wgrad(xs, ds, dh, wa, unmix):
    n_c = len(xs)
    n_e, _, _, dim = xs[0].shape
    wide, half = dh[0].shape[3], wa[0].shape[3]
    spec = lambda w: [pl.BlockSpec((1, 2, SEG, w), lambda e: (e, 0, 0, 0)) for _ in range(n_c)]
    return pl.pallas_call(
        functools.partial(wgrad_kernel, n_c),
        grid=(n_e,),
        in_specs=spec(dim) + spec(dim) + spec(wide) + spec(half) + [pl.BlockSpec((wide, wide), lambda e: (0, 0))],
        out_specs=[pl.BlockSpec((1, dim, wide), lambda e: (e, 0, 0)), pl.BlockSpec((1, half, dim), lambda e: (e, 0, 0))],
        out_shape=[jax.ShapeDtypeStruct((n_e, dim, wide), BF), jax.ShapeDtypeStruct((n_e, half, dim), BF)],
        scratch_shapes=[pltpu.VMEM((dim, wide), F32), pltpu.VMEM((half, dim), F32)],
        compiler_params=pltpu.CompilerParams(dimension_semantics=('arbitrary',), vmem_limit_bytes=64000 * 1024),
        cost_estimate=pl.CostEstimate(flops=26_000_000_000, bytes_accessed=100_000_000, transcendentals=0),
        name='weight_grads',
    )(*xs, *ds, *dh, *wa, unmix)


def solution(mesh):
    tp_count = mesh.shape['tp']
    ep_count = mesh.shape['ep']
    n_dev = tp_count * ep_count
    tok_spec = P(('ep', 'tp'), None)

    CORE, XF, YF = 2, 4, 1

    def flip(arr, bits):
        turned = (bits & 1) * ep_count + (bits >> 1)
        return lax.ppermute(arr, ('tp', 'ep'), [(s, s ^ turned) for s in range(n_dev)])

    def device_fn(x_loc, idx_loc, slot_loc, w_router, b_router, w_gate_up, b_gate_up, w_down, b_down, dy_loc):
        toks, dim = x_loc.shape
        n_experts = w_router.shape[1]
        n_e = w_gate_up.shape[0]
        wide = w_gate_up.shape[2]
        half = wide // 2
        tp_index = lax.axis_index('tp')
        ep_index = lax.axis_index('ep')
        me = ep_index * tp_count + tp_index

        logits = jnp.dot(x_loc, w_router, preferred_element_type=F32) + b_router[None, :]
        expert_hot = idx_loc[:, :, None] == jnp.arange(n_experts)[None, None, :]
        picked = jnp.sum(jnp.where(expert_hot, logits[:, None, :], 0.0), axis=2)
        gate_w = jax.nn.softmax(picked, axis=1)
        w_full = jnp.sum(jnp.where(expert_hot, gate_w[:, :, None], 0.0), axis=1)
        kept = jnp.any(expert_hot & (slot_loc >= 0)[:, :, None], axis=1)
        below = (jnp.arange(toks)[None, :] < jnp.arange(toks)[:, None]).astype(BF)
        rank = jnp.where(kept, jnp.dot(below, kept.astype(BF), preferred_element_type=F32), -1.0)
        aux = jnp.concatenate([w_full.T, rank.T], axis=0)

        xd = jnp.stack([x_loc, dy_loc])
        pairs = []
        for bits in (0, XF, YF, XF | YF):
            got, got_aux = (xd, aux) if bits == 0 else (flip(xd, bits), flip(aux, bits))
            pairs.append((bits, got, got_aux, flip(got, CORE), flip(got_aux, CORE)))

        col = jnp.arange(wide)
        split_mat = (jnp.where(col < half, 2 * col, 2 * (col - half) + 1)[None, :] == col[:, None]).astype(BF)
        w1 = jnp.einsum('edf,fg->edg', w_gate_up, split_mat, preferred_element_type=BF)
        w1t = jnp.einsum('edf,fg->egd', w_gate_up, split_mat, preferred_element_type=BF)
        w2t = jnp.swapaxes(w_down, 1, 2)
        b1 = jnp.concatenate([b_gate_up[:, 0::2], b_gate_up[:, 1::2]], axis=1)[:, None, :]
        b2 = (b_down * (tp_index == 0).astype(F32))[:, None, :]

        outs, dxs, dgs, gb1s, saved, w_all, kept_all = [], [], [], [], [], [], []
        for bits, xd_a, aux_a, xd_b, aux_b in pairs:
            x2 = jnp.stack([xd_a[0], xd_b[0]])
            d2 = jnp.stack([xd_a[1], xd_b[1]])
            both = jnp.stack([aux_a, aux_b], axis=1)
            wv = lax.dynamic_slice_in_dim(both, ep_index * n_e, n_e, axis=0)
            rk = lax.dynamic_slice_in_dim(both, n_experts + ep_index * n_e, n_e, axis=0)
            cnt = (jnp.max(rk, axis=2) + 1.0).astype(jnp.int32).reshape(-1)
            out2, dx2, dg2, gb1, xs, ds, dh, wa = run_chunk(cnt, x2, d2, rk, wv, w1, w1t, w_down, w2t, b1, b2)
            theirs = flip(jnp.stack([out2[1], dx2[1]]), CORE)
            mine = jnp.stack([out2[0], dx2[0]]).astype(F32) + theirs.astype(F32)
            if bits:
                mine = flip(mine.astype(BF), bits).astype(F32)
            outs.append(mine)
            dgs.append(dg2)
            gb1s.append(gb1)
            saved.append((xs, ds, dh, wa))
            wk = jnp.where(rk >= 0, wv, 0.0)
            w_all.append(wk)

        gw1, gw2 = run_wgrad(*[list(t) for t in zip(*saved)], split_mat.T)
        gb1 = functools.reduce(jnp.add, gb1s)[:, 0, :]
        gb1 = jnp.stack([gb1[:, :half], gb1[:, half:]], axis=2).reshape(n_e, wide)
        gb2 = 0.0
        for (bits, xd_a, _, xd_b, _), wk in zip(pairs, w_all):
            for k, xd_k in enumerate((xd_a, xd_b)):
                gb2 = gb2 + jnp.dot(wk[:, k, :], xd_k[1].astype(F32), precision=lax.Precision.HIGHEST)

        rel = [b | c for b in (0, XF, YF, XF | YF) for c in (0, CORE)]
        dg_rel = jnp.stack([dg[:, k, :] for dg in dgs for k in range(2)])
        slot_of = jnp.array([rel.index(m) for m in range(n_dev)], jnp.int32)
        dg_abs = dg_rel[slot_of[jnp.arange(n_dev) ^ me]]
        dg_back = lax.all_to_all(dg_abs, ('ep', 'tp'), 0, 0, tiled=True)
        d_gate = jnp.sum(dg_back.reshape(ep_count, tp_count, n_e, toks), axis=1).reshape(n_experts, toks).T
        d_logits = w_full * (d_gate - jnp.sum(w_full * d_gate, axis=1, keepdims=True))
        d_logits_b = d_logits.astype(BF)
        gwr = lax.psum(jnp.einsum('td,te->de', x_loc, d_logits_b, preferred_element_type=F32), ('tp', 'ep'))
        gbr = lax.psum(jnp.sum(d_logits, axis=0), ('tp', 'ep'))
        total = functools.reduce(jnp.add, outs)
        d_x = total[1] + jnp.einsum('te,de->td', d_logits_b, w_router, preferred_element_type=F32)
        return (total[0].astype(BF), d_x.astype(BF), gw1, gb1, gw2, gb2, gwr, gbr)

    in_specs = (tok_spec, tok_spec, tok_spec, P(None, None), P(None), P('ep', None, 'tp'), P('ep', 'tp'), P('ep', 'tp', None), P('ep', None), tok_spec)
    out_specs = (tok_spec, tok_spec, P('ep', None, 'tp'), P('ep', 'tp'), P('ep', 'tp', None), P('ep', None), P(None, None), P(None))
    return jax.shard_map(device_fn, mesh=mesh, in_specs=in_specs, out_specs=out_specs, check_vma=False)
```

time: 2920 us -> 533 us (0.18)
  waiting for transfers between devices: 2070 us -> 107 us
  matrix products: 364 us -> 27.3 us
  Pallas kernels: 0 us -> 221 us
  local copies, waits for them, and re-layouts: 256 us -> 64.6 us
  other arithmetic: 116 us -> 42.1 us
  starting transfers between devices: 65.4 us -> 30.8 us
    all_to_all x6 -> x1, waiting for transfers between devices: 1410 us -> 73.2 us  [device_fn(): dg_back = lax.all_to_all(dg_abs, ('ep', 'tp'), 0, 0, tiled=True)]
    all_gather x2 -> x0, waiting for transfers between devices: 667 us -> none  [dispatch(): lax.all_gather(buf_in.reshape(n_experts, capacity, model_dim), 'tp', axis=0)]
    dot_general x13, matrix products: 364 us -> 27.3 us  [the longest x8 12.8 us: device_fn(): jnp.dot(wk[:, k, :], xd_k[1].astype(F32), precision=lax.Precision.HIGHEST)]
    pallas_call x0 -> x5, Pallas kernels: none -> 221 us  [the longest x4 181 us: run_chunk(): pl.pallas_call(chunk_kernel, grid_spec=pltpu.PrefetchScalarGridSpec(num_s...]
    reduce_sum x7 -> x4, other arithmetic: 66.3 us -> 0.94 us  [the longest x1 0.78 us: device_fn(): w_full = jnp.sum(jnp.where(expert_hot, gate_w[:, :, None], 0.0), axis=1)]
    all_to_all x6 -> x1, starting transfers between devices: 65.2 us -> 2.11 us  [device_fn(): dg_back = lax.all_to_all(dg_abs, ('ep', 'tp'), 0, 0, tiled=True)]
    convert_element_type x3 -> x8, local copies, waits for them, and re-layouts: 56.5 us -> 3.87 us  [the longest x7 2.74 us: device_fn(): cnt = (jnp.max(rk, axis=2) + 1.0).astype(jnp.int32).reshape(-1)]
    all_to_all x2 -> x0, local copies, waits for them, and re-layouts: 45.3 us -> none  [collect(): lax.all_to_all(part_in.reshape(tp_count, n_experts, capacity, model_dim),...]
  transfers between devices with their start and end apart: 9 -> 23, of which waited for: 7 -> 4; matrix products, arithmetic and copies ran while one was open for 19% -> 23% of each run, Pallas kernels for 0% -> 42%
where the time goes in v1:
time: 533 us; the launch traced here: 531 us
  Pallas kernels  221 us (41%)
  waiting for transfers between devices  107 us (20%)
  local copies, waits for them, and re-layouts  64.6 us (12%)
  other arithmetic  42.1 us (8%)
  starting transfers between devices  30.8 us (6%)
  matrix products  27.3 us (5%)
  blocking collectives  23.4 us (4%)
  between operations  14.8 us (3%)
    pallas_call x4, Pallas kernels, run_chunk(): pl.pallas_call(chunk_kernel, grid_spec=pltpu.PrefetchScalarGridSpec(num_s...  181 us
    all_to_all x1, waiting for transfers between devices, device_fn(): dg_back = lax.all_to_all(dg_abs, ('ep', 'tp'), 0, 0, tiled=True)  73.2 us
    pallas_call x1, Pallas kernels, run_wgrad(): pl.pallas_call(functools.partial(wgrad_kernel, n_c), grid=(n_e,), in_spec...  40.3 us
    ppermute x21, starting transfers between devices, flip(): lax.ppermute(arr, ('tp', 'ep'), [(s, s ^ turned) for s in range(n_dev)])  28.7 us
    psum x1, blocking collectives, device_fn(): gbr = lax.psum(jnp.sum(d_logits, axis=0), ('tp', 'ep'))  23.4 us
    ppermute x21, waiting for transfers between devices, flip(): lax.ppermute(arr, ('tp', 'ep'), [(s, s ^ turned) for s in range(n_dev)])  22.8 us
    slice x8, local copies, waits for them, and re-layouts, device_fn(): mine = jnp.stack([out2[0], dx2[0]]).astype(F32) + theirs.astype(F32)  15.1 us
    slice x7, local copies, waits for them, and re-layouts, device_fn(): d2 = jnp.stack([xd_a[1], xd_b[1]])  13.3 us
  transfers between devices with their start and end apart: 23, of which 4 were waited for; matrix products, arithmetic and copies ran while one was open for 23% of the time, Pallas kernels for 42%

profile of v1, /device:TPU:0, one launch (start us, length us, event | category | flops | bytes accessed | tf_op | source)
XLA Modules:
  0.0 531.3 jit_solution(8518042127304469058)
XLA Ops:
  13.1 3.4 collective-permute-start.9
  21.0 10.2 %fusion.15 = bf16[512,8,1024]{2,0,1:T(8,128)(2,1)} fusion(bf16[8,1024,512]{2,1,0:T(8,128)(2,1)} %param.16, s32[512]{0:T(512)S(1)} %fusion.40), kind=kOutput, calls=%fused_computation.47 | convolution fusion | flops 4295229440 | bytes 16779264 | tf_op jit(solution)/shard_map/edf,fg->edg/dot_general | solution.py:247
  34.5 6.4 %copy.134 = bf16[8,256,1024]{1,2,0:T(8,128)(2,1)} copy(bf16[8,256,1024]{2,1,0:T(8,128)(2,1)} %w2_ref.7) | data formatting | bytes 8388608 | tf_op args[7]
  40.9 11.4 %copy.133 = bf16[512,8,1024]{0,2,1:T(8,128)(2,1)} copy(bf16[512,8,1024]{2,0,1:T(8,128)(2,1)} %fusion.15) | data formatting | bytes 16777216 | tf_op jit(solution)/shard_map/edf,fg->edg/dot_general | solution.py:247
  69.5 45.9 %experts.4 = (bf16[2,512,1024]{2,1,0:T(8,128)(2,1)}, bf16[2,512,1024]{2,1,0:T(8,128)(2,1)}, f32[8,2,512]{2,1,0:T(2,128)}, f32[8,1,512]{2,1,0:T(1,128)}, bf16[8,2...) custom-call(s32[16]{0:T(128)} %convert_element_type.98.cnt_ref, ...), custom_call_target="tpu_custom_call" | custom-call | flops 28000000000 | bytes 64000000 | tf_op jit(solution)/shard_map/experts/pallas_call | solution.py:120
  115.4 2.9 fusion.61
  123.4 22.6 %collective-permute-done.11 = bf16[2,512,1024]{2,1,0:T(8,128)(2,1)} collective-permute-done((bf16[2,512,1024]{2,1,0:T(8,128)(2,1)}, bf16[2,512,1024]{2,1,0:T(8,128)(2,1)}, u32[]{:S(2)}, u32[]{:S(2)}) %collective-permute-start.11) | collective-permute-done | bytes 2097184 | tf_op jit(solution)/shard_map/ppermute | solution.py:217
  155.8 3.1 fusion.70
  158.9 3.0 fusion.66
  165.6 45.1 %experts.7 = (bf16[2,512,1024]{2,1,0:T(8,128)(2,1)}, bf16[2,512,1024]{2,1,0:T(8,128)(2,1)}, f32[8,2,512]{2,1,0:T(2,128)}, f32[8,1,512]{2,1,0:T(1,128)}, bf16[8,2...) custom-call(s32[16]{0:T(128)} %convert_element_type.115.cnt_ref, ...), custom_call_target="tpu_custom_call" | custom-call | flops 28000000000 | bytes 64000000 | tf_op jit(solution)/shard_map/experts/pallas_call | solution.py:120
  222.1 45.5 %experts.6 = (bf16[2,512,1024]{2,1,0:T(8,128)(2,1)}, bf16[2,512,1024]{2,1,0:T(8,128)(2,1)}, f32[8,2,512]{2,1,0:T(2,128)}, f32[8,1,512]{2,1,0:T(1,128)}, bf16[8,2...) custom-call(s32[16]{0:T(128)} %convert_element_type.109.cnt_ref, ...), custom_call_target="tpu_custom_call" | custom-call | flops 28000000000 | bytes 64000000 | tf_op jit(solution)/shard_map/experts/pallas_call | solution.py:120
  267.6 2.9 fusion.68
  279.4 44.4 %experts.5 = (bf16[2,512,1024]{2,1,0:T(8,128)(2,1)}, bf16[2,512,1024]{2,1,0:T(8,128)(2,1)}, f32[8,2,512]{2,1,0:T(2,128)}, f32[8,1,512]{2,1,0:T(1,128)}, bf16[8,2...) custom-call(s32[16]{0:T(128)} %convert_element_type.103.cnt_ref, ...), custom_call_target="tpu_custom_call" | custom-call | flops 28000000000 | bytes 64000000 | tf_op jit(solution)/shard_map/experts/pallas_call | solution.py:120
  323.9 2.9 fusion.64
  332.1 40.3 %weight_grads.1 = (bf16[8,1024,512]{2,1,0:T(8,128)(2,1)}, bf16[8,256,1024]{2,1,0:T(8,128)(2,1)}) custom-call(bf16[8,2,256,1024]{3,2,1,0:T(8,128)(2,1)} %get-tuple-element.54.refs_0_, bf16[8,2,256,1024]{3,2,1,0:T(8,128)(2,1)} %get-tuple-element.55.refs_1_, bf16[8,2,256,1024]{3,2,1,0:T(8,128)(2,1)} %get-tuple-element.56.refs_2_, ...), custom_call_target="tpu_custom_call" | custom-call | flops 25999998976 | bytes 100000000 | tf_op jit(solution)/shard_map/weight_grads/pallas_call | solution.py:194
  372.4 4.3 add_convert_fusion
  376.8 7.1 %collective-permute-start.20 = (bf16[2,512,1024]{2,1,0:T(8,128)(2,1)}, bf16[2,512,1024]{2,1,0:T(8,128)(2,1)}, u32[]{:S(2)}, u32[]{:S(2)}) collective-permute-start(bf16[2,512,1024]{2,1,0:T(8,128)(2,1)} %add_convert_fusion), channel_id=1, source_target_pairs={{0,6},{1,7},{2,4},{3,5},{4,2},{5,3},{6,0},{7,1}} | collective-permute-start | bytes 6291464 | tf_op jit(solution)/shard_map/ppermute | solution.py:217
  383.9 4.0 add_convert_fusion.1
  388.0 2.8 collective-permute-start.14
  390.8 3.9 add_convert_fusion.2
  404.9 73.2 %all-to-all-done = f32[8,8,512]{2,1,0:T(8,128)S(1)} async-done(((f32[8,8,512]{2,1,0:T(8,128)}), f32[8,8,512]{2,1,0:T(8,128)S(1)}, u32[]{:S(2)}, u32[]{:S(2)}) %all-to-all-start) | async-done | bytes 131104 | tf_op jit(solution)/shard_map/all_to_all | solution.py:285
  479.2 23.4 %psum.15 = f32[32]{0:T(128)} all-reduce(f32[32]{0:T(128)S(1)} %get-tuple-element.158), channel_id=1, replica_groups=mesh['tp'=2,'ep'=4] {'tp','ep'}, use_global_device_ids=true, to_apply=%region_13.14 | all-reduce | flops 32 | bytes 256 | tf_op jit(solution)/shard_map/psum | solution.py:290
  502.6 6.4 %convert_add_fusion = f32[2,512,1024]{2,1,0:T(8,128)S(1)} fusion(bf16[2,512,1024]{2,1,0:T(8,128)(2,1)} %collective-permute-done.20, bf16[2,512,1024]{2,1,0:T(8,128)(2,1)} %collective-permute-done.14, bf16[2,512,1024]{2,1,0:T(8,128)(2,1)} %collective-permute-done.8, bf16[2,512,1024]{2,1,0:T(8,128)(2,1)} %collective-permute-done.2, ...), kind=kLoop, calls=%fused_computation.2 | loop fusion | flops 10485760 | bytes 14680064 | tf_op jit(solution)/shard_map/add | solution.py:291
  511.6 11.0 %all-reduce.2.cloned.1.call-done = f32[1024,32]{0,1:T(8,128)} async-done(((f32[1024,32]{0,1:T(8,128)}), f32[1024,32]{0,1:T(8,128)}) %all-reduce.2.cloned.1.call-update) | async-done | bytes 131088 | tf_op jit(solution)/shard_map/psum | solution.py:289
  (207 shorter events, 90.3 us)
Async XLA Ops:
  13.1 41.9 %collective-permute-start.9 = (f32[64,512]{1,0:T(8,128)S(1)}, f32[64,512]{1,0:T(8,128)S(1)}, u32[]{:S(2)}, u32[]{:S(2)}) collective-permute-start(f32[64,512]{1,0:T(8,128)S(1)} %get-tuple-element.161), channel_id=1, source_target_pairs={{0,4},{1,5},{2,6},{3,7},{4,0},{5,1},{6,2},{7,3}} | collective-permute-start | bytes 393224 | tf_op jit(solution)/shard_map/ppermute | solution.py:217
  16.5 38.6 %collective-permute-start.3 = (f32[64,512]{1,0:T(8,128)S(1)}, f32[64,512]{1,0:T(8,128)S(1)}, u32[]{:S(2)}, u32[]{:S(2)}) collective-permute-start(f32[64,512]{1,0:T(8,128)S(1)} %get-tuple-element.161), channel_id=1, source_target_pairs={{0,2},{1,3},{2,0},{3,1},{4,6},{5,7},{6,4},{7,5}} | collective-permute-start | bytes 393224 | tf_op jit(solution)/shard_map/ppermute | solution.py:217
  18.0 34.3 %collective-permute-start = (f32[64,512]{1,0:T(8,128)S(1)}, f32[64,512]{1,0:T(8,128)S(1)}, u32[]{:S(2)}, u32[]{:S(2)}) collective-permute-start(f32[64,512]{1,0:T(8,128)S(1)} %get-tuple-element.161), channel_id=1, source_target_pairs={{0,1},{1,0},{2,3},{3,2},{4,5},{5,4},{6,7},{7,6}} | collective-permute-start | bytes 393224 | tf_op jit(solution)/shard_map/ppermute | solution.py:217
  18.0 40.1 %collective-permute-start.15 = (f32[64,512]{1,0:T(8,128)S(1)}, f32[64,512]{1,0:T(8,128)S(1)}, u32[]{:S(2)}, u32[]{:S(2)}) collective-permute-start(f32[64,512]{1,0:T(8,128)S(1)} %get-tuple-element.161), channel_id=1, source_target_pairs={{0,6},{1,7},{2,4},{3,5},{4,2},{5,3},{6,0},{7,1}} | collective-permute-start | bytes 393224 | tf_op jit(solution)/shard_map/ppermute | solution.py:217
  19.5 45.9 %collective-permute-start.1 = (bf16[2,512,1024]{2,1,0:T(8,128)(2,1)}, bf16[2,512,1024]{2,1,0:T(8,128)(2,1)}, u32[]{:S(2)}, u32[]{:S(2)}) collective-permute-start(bf16[2,512,1024]{2,1,0:T(8,128)(2,1)} %pad_maximum_fusion), channel_id=1, source_target_pairs={{0,1},{1,0},{2,3},{3,2},{4,5},{5,4},{6,7},{7,6}} | collective-permute-start | bytes 6291464 | tf_op jit(solution)/shard_map/ppermute | solution.py:217
  52.3 71.0 %collective-permute-start.17 = (bf16[2,512,1024]{2,1,0:T(8,128)(2,1)}, bf16[2,512,1024]{2,1,0:T(8,128)(2,1)}, u32[]{:S(2)}, u32[]{:S(2)}) collective-permute-start(bf16[2,512,1024]{2,1,0:T(8,128)(2,1)} %pad_maximum_fusion), channel_id=1, source_target_pairs={{0,6},{1,7},{2,4},{3,5},{4,2},{5,3},{6,0},{7,1}} | collective-permute-start | bytes 6291464 | tf_op jit(solution)/shard_map/ppermute | solution.py:217
  55.1 3.7 collective-permute-start.10
  55.1 4.8 collective-permute-start.4
  58.1 87.9 %collective-permute-start.11 = (bf16[2,512,1024]{2,1,0:T(8,128)(2,1)}, bf16[2,512,1024]{2,1,0:T(8,128)(2,1)}, u32[]{:S(2)}, u32[]{:S(2)}) collective-permute-start(bf16[2,512,1024]{2,1,0:T(8,128)(2,1)} %pad_maximum_fusion), channel_id=1, source_target_pairs={{0,4},{1,5},{2,6},{3,7},{4,0},{5,1},{6,2},{7,3}} | collective-permute-start | bytes 6291464 | tf_op jit(solution)/shard_map/ppermute | solution.py:217
  58.8 87.6 %collective-permute-start.5 = (bf16[2,512,1024]{2,1,0:T(8,128)(2,1)}, bf16[2,512,1024]{2,1,0:T(8,128)(2,1)}, u32[]{:S(2)}, u32[]{:S(2)}) collective-permute-start(bf16[2,512,1024]{2,1,0:T(8,128)(2,1)} %pad_maximum_fusion), channel_id=1, source_target_pairs={{0,2},{1,3},{2,0},{3,1},{4,6},{5,7},{6,4},{7,5}} | collective-permute-start | bytes 6291464 | tf_op jit(solution)/shard_map/ppermute | solution.py:217
  59.9 3.5 collective-permute-start.16
  121.1 381.5 %collective-permute-start.2 = (bf16[2,512,1024]{2,1,0:T(8,128)(2,1)}, bf16[2,512,1024]{2,1,0:T(8,128)(2,1)}, u32[]{:S(2)}, u32[]{:S(2)}) collective-permute-start(bf16[2,512,1024]{2,1,0:T(8,128)(2,1)} %pad_maximum_fusion.3), channel_id=1, source_target_pairs={{0,1},{1,0},{2,3},{3,2},{4,5},{5,4},{6,7},{7,6}} | collective-permute-start | bytes 6291464 | tf_op jit(solution)/shard_map/ppermute | solution.py:217
  123.4 38.6 %collective-permute-start.18 = (bf16[2,512,1024]{2,1,0:T(8,128)(2,1)}, bf16[2,512,1024]{2,1,0:T(8,128)(2,1)S(1)}, u32[]{:S(2)}, u32[]{:S(2)}) collective-permute-start(bf16[2,512,1024]{2,1,0:T(8,128)(2,1)} %collective-permute-done.17), channel_id=1, source_target_pairs={{0,1},{1,0},{2,3},{3,2},{4,5},{5,4},{6,7},{7,6}} | collective-permute-start | bytes 6291464 | tf_op jit(solution)/shard_map/ppermute | solution.py:217
  146.0 72.0 %collective-permute-start.12 = (bf16[2,512,1024]{2,1,0:T(8,128)(2,1)}, bf16[2,512,1024]{2,1,0:T(8,128)(2,1)}, u32[]{:S(2)}, u32[]{:S(2)}) collective-permute-start(bf16[2,512,1024]{2,1,0:T(8,128)(2,1)} %collective-permute-done.11), channel_id=1, source_target_pairs={{0,1},{1,0},{2,3},{3,2},{4,5},{5,4},{6,7},{7,6}} | collective-permute-start | bytes 6291464 | tf_op jit(solution)/shard_map/ppermute | solution.py:217
  146.4 128.5 %collective-permute-start.6 = (bf16[2,512,1024]{2,1,0:T(8,128)(2,1)}, bf16[2,512,1024]{2,1,0:T(8,128)(2,1)}, u32[]{:S(2)}, u32[]{:S(2)}) collective-permute-start(bf16[2,512,1024]{2,1,0:T(8,128)(2,1)} %collective-permute-done.5), channel_id=1, source_target_pairs={{0,1},{1,0},{2,3},{3,2},{4,5},{5,4},{6,7},{7,6}} | collective-permute-start | bytes 6291464 | tf_op jit(solution)/shard_map/ppermute | solution.py:217
  215.7 156.7 %collective-permute-start.19 = (bf16[2,512,1024]{2,1,0:T(8,128)(2,1)}, bf16[2,512,1024]{2,1,0:T(8,128)(2,1)}, u32[]{:S(2)}, u32[]{:S(2)}) collective-permute-start(bf16[2,512,1024]{2,1,0:T(8,128)(2,1)} %pad_maximum_fusion.12), channel_id=1, source_target_pairs={{0,1},{1,0},{2,3},{3,2},{4,5},{5,4},{6,7},{7,6}} | collective-permute-start | bytes 6291464 | tf_op jit(solution)/shard_map/ppermute | solution.py:217
  273.1 110.9 %collective-permute-start.13 = (bf16[2,512,1024]{2,1,0:T(8,128)(2,1)}, bf16[2,512,1024]{2,1,0:T(8,128)(2,1)}, u32[]{:S(2)}, u32[]{:S(2)}) collective-permute-start(bf16[2,512,1024]{2,1,0:T(8,128)(2,1)} %pad_maximum_fusion.9), channel_id=1, source_target_pairs={{0,1},{1,0},{2,3},{3,2},{4,5},{5,4},{6,7},{7,6}} | collective-permute-start | bytes 6291464 | tf_op jit(solution)/shard_map/ppermute | solution.py:217
  329.5 61.3 %collective-permute-start.7 = (bf16[2,512,1024]{2,1,0:T(8,128)(2,1)}, bf16[2,512,1024]{2,1,0:T(8,128)(2,1)}, u32[]{:S(2)}, u32[]{:S(2)}) collective-permute-start(bf16[2,512,1024]{2,1,0:T(8,128)(2,1)} %pad_maximum_fusion.6), channel_id=1, source_target_pairs={{0,1},{1,0},{2,3},{3,2},{4,5},{5,4},{6,7},{7,6}} | collective-permute-start | bytes 6291464 | tf_op jit(solution)/shard_map/ppermute | solution.py:217
  376.8 125.8 %collective-permute-start.20 = (bf16[2,512,1024]{2,1,0:T(8,128)(2,1)}, bf16[2,512,1024]{2,1,0:T(8,128)(2,1)}, u32[]{:S(2)}, u32[]{:S(2)}) collective-permute-start(bf16[2,512,1024]{2,1,0:T(8,128)(2,1)} %add_convert_fusion), channel_id=1, source_target_pairs={{0,6},{1,7},{2,4},{3,5},{4,2},{5,3},{6,0},{7,1}} | collective-permute-start | bytes 6291464 | tf_op jit(solution)/shard_map/ppermute | solution.py:217
  388.0 114.6 %collective-permute-start.14 = (bf16[2,512,1024]{2,1,0:T(8,128)(2,1)}, bf16[2,512,1024]{2,1,0:T(8,128)(2,1)}, u32[]{:S(2)}, u32[]{:S(2)}) collective-permute-start(bf16[2,512,1024]{2,1,0:T(8,128)(2,1)} %add_convert_fusion.1), channel_id=1, source_target_pairs={{0,4},{1,5},{2,6},{3,7},{4,0},{5,1},{6,2},{7,3}} | collective-permute-start | bytes 6291464 | tf_op jit(solution)/shard_map/ppermute | solution.py:217
  394.7 107.9 %collective-permute-start.8 = (bf16[2,512,1024]{2,1,0:T(8,128)(2,1)}, bf16[2,512,1024]{2,1,0:T(8,128)(2,1)}, u32[]{:S(2)}, u32[]{:S(2)}) collective-permute-start(bf16[2,512,1024]{2,1,0:T(8,128)(2,1)} %add_convert_fusion.2), channel_id=1, source_target_pairs={{0,2},{1,3},{2,0},{3,1},{4,6},{5,7},{6,4},{7,5}} | collective-permute-start | bytes 6291464 | tf_op jit(solution)/shard_map/ppermute | solution.py:217
  397.0 81.0 %all-to-all-start = ((f32[8,8,512]{2,1,0:T(8,128)}), f32[8,8,512]{2,1,0:T(8,128)S(1)}, u32[]{:S(2)}, u32[]{:S(2)}) async-start(f32[8,8,512]{2,1,0:T(8,128)} %gather_fusion.1), calls=%async_computation | async-start | bytes 262144 | tf_op jit(solution)/shard_map/all_to_all | solution.py:285
  399.2 79.0 %copy-start.3 = (bf16[512,1024]{1,0:T(8,128)(2,1)S(1)}, bf16[512,1024]{1,0:T(8,128)(2,1)}, u32[]{:S(2)}) copy-start(bf16[512,1024]{1,0:T(8,128)(2,1)} %param.11) | copy-start | bytes 3145732
  399.2 123.5 %all-reduce.2.cloned.1.call-start = ((), (), s32[]{:S(2)}) async-start(), calls=%async_computation.1 | async-start | bytes 262144 | tf_op jit(solution)/shard_map/psum | solution.py:289
  (33 other events, 275.8 us)
Sparse Core Ops, SparseCore 0:
  479.3 43.3 all-reduce.1

commit v2 on v0

v2 whole, which is shorter than its diff:
```python
import functools
import jax
import jax.numpy as jnp
from jax import lax
from jax.experimental import pallas as pl
from jax.experimental.pallas import tpu as pltpu
from jax.sharding import PartitionSpec as P

LIMIT = 7.0
ALPHA = 1.702
BF = jnp.bfloat16
F32 = jnp.float32
TILE = 256
SIZES = (128, 256)
BACK = ((1,), (1,))
LHS = ((0,), (0,))


def dot(a, b, dims=((1,), (0,))):
    return lax.dot_general(a, b, (dims, ((), ())), preferred_element_type=F32)


def chunk_kernel(first, toks, ep_ref, xa_ref, xb_ref, w1_in, w2_ref, b1_ref, b2_ref, *refs):
    if first:
        split_ref, *refs = refs
    oa_ref, ob_ref, dg_ref, gb1_ref, gb2_ref, nt_ref, *refs = refs
    if first:
        w1_ref, *refs = refs
    else:
        w1_ref = w1_in
    xs_hbm, ds_hbm, dh_hbm, wa_hbm, *refs = refs
    aux, xbuf, dbuf, dhst, wast, wrow, dgrow, yst, dxst, sel, ybuf, dxbuf, acc, off, sems = refs
    e = pl.program_id(0)
    n_e = pl.num_programs(0)
    half = w2_ref.shape[1]
    tok_refs = (xa_ref, xb_ref)
    par = lax.rem(e, 2)

    def saves(expert, t, p):
        at = pl.ds(t * TILE, TILE)
        pairs = ((xbuf, xs_hbm), (dbuf, ds_hbm), (dhst, dh_hbm), (wast, wa_hbm))
        return [pltpu.make_async_copy(src.at[p, at], dst.at[expert, t], sems.at[p, t, k])
                for k, (src, dst) in enumerate(pairs)]

    def drain(expert, p):
        for t in range(2):
            @pl.when(nt_ref[expert] > t)
            def _():
                for copy in saves(expert, t, p):
                    copy.wait()

    @pl.when(e == 0)
    def _():
        for i in range(2):
            off[i] = 0
            aux[i] = tok_refs[i][2 * toks:, :].astype(F32)
            xbuf[i] = jnp.zeros(xbuf.shape[1:], BF)
            dbuf[i] = jnp.zeros(dbuf.shape[1:], BF)
        yst[...] = jnp.zeros_like(yst)
        dxst[...] = jnp.zeros_like(dxst)

    for p in range(2):
        @pl.when((e >= 2) & (par == p))
        def _():
            drain(e - 2, p)

    if first:
        w1_ref[0] = dot(w1_in[0], split_ref[...]).astype(BF)

    row = ep_ref[0] * n_e + e
    wrow[...] = jnp.zeros_like(wrow)
    ranks, counts = [], []
    for i in range(2):
        rk = aux[i, pl.ds(row + 4 * n_e, 1), :][:, toks:]
        ranks.append(rk)
        counts.append((jnp.max(rk) + 1.0).astype(jnp.int32))
    starts = (0, pl.multiple_of((counts[0] + 15) // 16 * 16, 16))
    n_tiles = (starts[1] + counts[1] + TILE - 1) // TILE
    nt_ref[e] = n_tiles

    def place(i, m):
        pair = aux[i, pl.ds(row, 1), :]
        low = aux[i, pl.ds(row + 4 * n_e, 1), :]
        wv = pair[:, :toks] + pair[:, toks:] + low[:, :toks]
        pos = lax.broadcasted_iota(jnp.int32, (m, toks), 0).astype(F32)
        hot = jnp.broadcast_to(ranks[i], (m, toks)) == pos
        hot_b = jnp.where(hot, 1.0, 0.0).astype(BF)
        at = pl.ds(starts[i], m)
        wrow[at, :] = jnp.sum(jnp.where(hot, jnp.broadcast_to(wv, (m, toks)), 0.0), axis=1, keepdims=True)
        xbuf[par, at, :] = dot(hot_b, tok_refs[i][:toks, :]).astype(BF)
        dbuf[par, at, :] = dot(hot_b, tok_refs[i][toks:2 * toks, :]).astype(BF)
        sel[i, pl.ds(pl.multiple_of(off[i], 128), m), :] = hot_b

    for i in range(2):
        low = 0
        for m in SIZES:
            pl.when((counts[i] > low) & (counts[i] <= m))(functools.partial(place, i, m))
            low = m

    gb1_ref[...] = jnp.zeros_like(gb1_ref)
    gb2_ref[...] = jnp.zeros_like(gb2_ref)

    def tile(t, _):
        at = pl.ds(pl.multiple_of(t * TILE, TILE), TILE)
        x_rows = xbuf[par, at, :]
        d_rows = dbuf[par, at, :]
        w_row = wrow[at, :]
        hid = dot(x_rows, w1_ref[0]) + b1_ref[0]
        gate, up = hid[:, :half], hid[:, half:]
        g = jnp.minimum(gate, LIMIT)
        u1 = jnp.clip(up, -LIMIT, LIMIT) + 1.0
        sg = jax.nn.sigmoid(ALPHA * g)
        gs = g * sg
        act = (gs * u1).astype(BF)
        part = (dot(act, w2_ref[0]) + b2_ref[0]).astype(BF).astype(F32)
        d_wide = d_rows.astype(F32)
        dgrow[at, :] = jnp.sum(part * d_wide, axis=1, keepdims=True)
        gb2_ref[0] += jnp.sum(w_row * d_wide, axis=0, keepdims=True)
        yst[at, :] = (w_row * part).astype(BF)
        d_act = w_row * dot(d_rows, w2_ref[0], BACK)
        gate_on = jnp.where(gate < LIMIT, 1.0, jnp.where(gate == LIMIT, 0.5, 0.0))
        up_abs = jnp.abs(up)
        up_on = jnp.where(up_abs < LIMIT, 1.0, jnp.where(up_abs == LIMIT, 0.5, 0.0))
        d_gate = d_act * u1 * (sg * (1.0 + ALPHA * g * (1.0 - sg))) * gate_on
        d_up = d_act * gs * up_on
        d_hid = jnp.concatenate([d_gate, d_up], axis=1)
        gb1_ref[0] += jnp.sum(d_hid, axis=0, keepdims=True)
        d_hid_b = d_hid.astype(BF)
        dhst[par, at, :] = d_hid_b
        wast[par, at, :] = (w_row * act.astype(F32)).astype(BF)
        dxst[at, :] = dot(d_hid_b, w1_ref[0], BACK).astype(BF)
        for copy in saves(e, t, par):
            copy.start()
        return 0

    lax.fori_loop(0, n_tiles, tile, 0)

    def collect(i, m):
        src = pl.ds(starts[i], m)
        dst = pl.ds(pl.multiple_of(off[i], 128), m)
        ybuf[i, dst, :] = yst[src, :]
        dxbuf[i, dst, :] = dxst[src, :]
        pos = lax.broadcasted_iota(jnp.int32, (m, toks), 0).astype(F32)
        hot = jnp.broadcast_to(ranks[i], (m, toks)) == pos
        dg_ref[0, i:i + 1, :] = jnp.sum(jnp.where(hot, dgrow[src, :], 0.0), axis=0, keepdims=True)
        off[i] = off[i] + m

    low = 0
    for m in SIZES:
        for i in range(2):
            pl.when((counts[i] > low) & (counts[i] <= m))(functools.partial(collect, i, m))
        low = m
    for i in range(2):
        @pl.when(counts[i] == 0)
        def _():
            dg_ref[0, i:i + 1, :] = jnp.zeros((1, toks), F32)

    @pl.when(e == n_e - 1)
    def _():
        for i, o_ref in enumerate((oa_ref, ob_ref)):
            total = pl.multiple_of(off[i], 128)
            for buf in (sel, ybuf, dxbuf):
                buf[i, pl.ds(total, TILE), :] = jnp.zeros((TILE, buf.shape[2]), BF)
            tiles = (total + TILE - 1) // TILE
            for k, buf in enumerate((ybuf, dxbuf)):
                acc[...] = jnp.zeros_like(acc)

                def step(j, _):
                    at = pl.ds(pl.multiple_of(j * TILE, TILE), TILE)
                    acc[...] += dot(sel[i, at, :], buf[i, at, :], LHS)
                    return 0

                lax.fori_loop(0, tiles, step, 0)
                o_ref[k * toks:(k + 1) * toks, :] = acc[...].astype(BF)
        for back in (1, 0):
            p = lax.rem(e - back, 2)
            drain(e - back, p)


def run_chunk(ep, xa, xb, w1, w2, b1, b2, toks, split=None):
    first = split is not None
    n_e, dim, wide = w1.shape
    half = w2.shape[1]
    whole = lambda e, ep: (0, 0)
    per_e = lambda e, ep: (e, 0, 0)
    once = dict(pipeline_mode=pl.Buffered(1))
    room = n_e * TILE + TILE
    hbm = pl.BlockSpec(memory_space=pl.ANY)
    in_specs = [
        pl.BlockSpec(xa.shape, whole, **once),
        pl.BlockSpec(xb.shape, whole, **once),
        pl.BlockSpec((1, dim, wide), per_e),
        pl.BlockSpec((1, half, dim), per_e),
        pl.BlockSpec((1, 1, wide), per_e),
        pl.BlockSpec((1, 1, dim), per_e),
    ]
    out_specs = [
        pl.BlockSpec((2 * toks, dim), whole, **once),
        pl.BlockSpec((2 * toks, dim), whole, **once),
        pl.BlockSpec((1, 2, toks), per_e),
        pl.BlockSpec((1, 1, wide), per_e),
        pl.BlockSpec((1, 1, dim), per_e),
        pl.BlockSpec(memory_space=pltpu.SMEM),
    ]
    shape = jax.ShapeDtypeStruct
    out_shape = [
        shape((2 * toks, dim), BF), shape((2 * toks, dim), BF), shape((n_e, 2, toks), F32),
        shape((n_e, 1, wide), F32), shape((n_e, 1, dim), F32), shape((n_e,), jnp.int32),
    ]
    if first:
        in_specs.append(pl.BlockSpec((wide, wide), whole))
        out_specs.append(pl.BlockSpec((1, dim, wide), per_e))
        out_shape.append(shape((n_e, dim, wide), BF))
    out_specs += [hbm] * 4
    out_shape += [shape((n_e, 2, TILE, w), BF) for w in (dim, dim, wide, half)]
    got = pl.pallas_call(
        functools.partial(chunk_kernel, first, toks),
        grid_spec=pltpu.PrefetchScalarGridSpec(
            num_scalar_prefetch=1,
            grid=(n_e,),
            in_specs=in_specs,
            out_specs=out_specs,
            scratch_shapes=[
                pltpu.VMEM((2, xa.shape[0] - 2 * toks, dim), F32),
                pltpu.VMEM((2, 2 * TILE, dim), BF),
                pltpu.VMEM((2, 2 * TILE, dim), BF),
                pltpu.VMEM((2, 2 * TILE, wide), BF),
                pltpu.VMEM((2, 2 * TILE, half), BF),
                pltpu.VMEM((2 * TILE, 1), F32),
                pltpu.VMEM((2 * TILE, 1), F32),
                pltpu.VMEM((2 * TILE, dim), BF),
                pltpu.VMEM((2 * TILE, dim), BF),
                pltpu.VMEM((2, room, toks), BF),
                pltpu.VMEM((2, room, dim), BF),
                pltpu.VMEM((2, room, dim), BF),
                pltpu.VMEM((toks, dim), F32),
                pltpu.SMEM((2,), jnp.int32),
                pltpu.SemaphoreType.DMA((2, 2, 4)),
            ],
        ),
        out_shape=out_shape,
        compiler_params=pltpu.CompilerParams(dimension_semantics=('arbitrary',), vmem_limit_bytes=65000 * 1024),
        cost_estimate=pl.CostEstimate(flops=28_000_000_000, bytes_accessed=40_000_000, transcendentals=0),
        name='experts',
    )(ep, xa, xb, w1, w2, b1, b2, *((split,) if first else ()))
    oa, ob, dg, gb1, gb2, nt = got[:6]
    return oa, ob, dg, gb1, gb2, nt, got[-4:], (got[6] if first else w1)


def wgrad_kernel(n_c, first_e, nt_ref, *refs):
    hbm = [refs[k * n_c:(k + 1) * n_c] for k in range(4)]
    mix_ref, gw1_ref, gw2_ref, acc1, acc2, *bufs, sems = refs[4 * n_c:]
    e = pl.program_id(0)
    n_e = pl.num_programs(0)
    par = lax.rem(e, 2)

    def fetches(step, c, t, p):
        return [pltpu.make_async_copy(hbm[k][c].at[first_e + step, t], bufs[k].at[p, 2 * c + t], sems.at[p, 2 * c + t, k])
                for k in range(4)]

    def each(step, act):
        for c in range(n_c):
            for t in range(2):
                pl.when(nt_ref[c, first_e + step] > t)(functools.partial(act, c, t))

    def start(step, p):
        def go(c, t):
            for copy in fetches(step, c, t, p):
                copy.start()
        each(step, go)

    @pl.when(e == 0)
    def _():
        start(e, par)

    @pl.when(e + 1 < n_e)
    def _():
        start(e + 1, 1 - par)

    acc1[...] = jnp.zeros_like(acc1)
    acc2[...] = jnp.zeros_like(acc2)

    def add(c, t):
        for copy in fetches(e, c, t, par):
            copy.wait()
        x_rows, d_rows, d_hid, act_w = (buf[par, 2 * c + t] for buf in bufs)
        acc1[...] += dot(x_rows, d_hid, LHS)
        acc2[...] += dot(act_w, d_rows, LHS)

    each(e, add)
    gw2_ref[0] = acc2[...].astype(BF)
    gw1_ref[0] = dot(acc1[...].astype(BF), mix_ref[...]).astype(BF)


def run_wgrad(nt, saved, unmix, first_e, n_e):
    n_c = len(saved)
    xs, ds, dh, wa = (list(t) for t in zip(*saved))
    dim, wide, half = xs[0].shape[3], dh[0].shape[3], wa[0].shape[3]
    return pl.pallas_call(
        functools.partial(wgrad_kernel, n_c, first_e),
        grid_spec=pltpu.PrefetchScalarGridSpec(
            num_scalar_prefetch=1,
            grid=(n_e,),
            in_specs=[pl.BlockSpec(memory_space=pl.ANY)] * (4 * n_c) + [pl.BlockSpec((wide, wide), lambda e, nt: (0, 0))],
            out_specs=[pl.BlockSpec((1, dim, wide), lambda e, nt: (e, 0, 0)), pl.BlockSpec((1, half, dim), lambda e, nt: (e, 0, 0))],
            scratch_shapes=[pltpu.VMEM((dim, wide), F32), pltpu.VMEM((half, dim), F32)]
            + [pltpu.VMEM((2, 2 * n_c, TILE, w), BF) for w in (dim, dim, wide, half)]
            + [pltpu.SemaphoreType.DMA((2, 2 * n_c, 4))],
        ),
        out_shape=[jax.ShapeDtypeStruct((n_e, dim, wide), BF), jax.ShapeDtypeStruct((n_e, half, dim), BF)],
        compiler_params=pltpu.CompilerParams(dimension_semantics=('arbitrary',), vmem_limit_bytes=64000 * 1024),
        cost_estimate=pl.CostEstimate(flops=26_000_000_000, bytes_accessed=60_000_000, transcendentals=0),
        name='weight_grads',
    )(nt, *xs, *ds, *dh, *wa, unmix)


def solution(mesh):
    tp_count = mesh.shape['tp']
    ep_count = mesh.shape['ep']
    n_dev = tp_count * ep_count
    tok_spec = P(('ep', 'tp'), None)

    CORE, XF, YF = 2, 4, 1
    CHIPS = (0, XF, YF | CORE, XF | YF)

    def flip(arr, bits):
        turned = (bits & 1) * ep_count + (bits >> 1)
        return lax.ppermute(arr, ('tp', 'ep'), [(s, s ^ turned) for s in range(n_dev)])

    def device_fn(x_loc, idx_loc, slot_loc, w_router, b_router, w_gate_up, b_gate_up, w_down, b_down, dy_loc):
        toks, dim = x_loc.shape
        n_experts = w_router.shape[1]
        n_e = w_gate_up.shape[0]
        wide = w_gate_up.shape[2]
        half = wide // 2
        tp_index = lax.axis_index('tp')
        ep_index = lax.axis_index('ep')
        me = ep_index * tp_count + tp_index

        logits = jnp.dot(x_loc, w_router, preferred_element_type=F32) + b_router[None, :]
        expert_hot = idx_loc[:, :, None] == jnp.arange(n_experts)[None, None, :]
        picked = jnp.sum(jnp.where(expert_hot, logits[:, None, :], 0.0), axis=2)
        gate_w = jax.nn.softmax(picked, axis=1)
        w_full = jnp.sum(jnp.where(expert_hot, gate_w[:, :, None], 0.0), axis=1)
        kept = jnp.any(expert_hot & (slot_loc >= 0)[:, :, None], axis=1)
        below = (jnp.arange(toks)[None, :] < jnp.arange(toks)[:, None]).astype(BF)
        rank = jnp.where(kept, jnp.dot(below, kept.astype(BF), preferred_element_type=F32), -1.0)
        w_top = lax.reduce_precision(w_full, 8, 7)
        w_mid = lax.reduce_precision(w_full - w_top, 8, 7)
        w_low = w_full - w_top - w_mid
        aux = jnp.concatenate([
            jnp.concatenate([w_top.T, w_mid.T], axis=1),
            jnp.concatenate([w_low.T, rank.T], axis=1)], axis=0).astype(BF)
        load = jnp.concatenate([x_loc, dy_loc, aux], axis=0)

        pairs = []
        for bits in CHIPS:
            got = load if bits == 0 else flip(load, bits)
            pairs.append((bits, got, flip(got, CORE)))

        col = jnp.arange(wide)
        split_mat = (jnp.where(col < half, 2 * col, 2 * (col - half) + 1)[None, :] == col[:, None]).astype(BF)
        b1 = jnp.concatenate([b_gate_up[:, 0::2], b_gate_up[:, 1::2]], axis=1)[:, None, :]
        b2 = (b_down * (tp_index == 0).astype(F32))[:, None, :]
        ep = ep_index.astype(jnp.int32)[None]

        w1 = w_gate_up
        outs, dgs, gb1s, gb2s, nts, saved = [], [], [], [], [], []
        pending = []

        def second_hop(bits, oa, theirs):
            mine = oa.astype(F32) + theirs.astype(F32)
            return mine.astype(BF) if bits else mine

        for step, (bits, xa, xb) in enumerate(pairs):
            if len(pending) == 2:
                b, oa_p, th_p = pending.pop(0)
                mine = second_hop(b, oa_p, th_p)
                mine, xa = lax.optimization_barrier((mine, xa))
                outs.append(flip(mine, b) if b else mine)
            oa, ob, dg, gb1, gb2, nt, keep, w1 = run_chunk(
                ep, xa, xb, w1, w_down, b1, b2, toks, split_mat if step == 0 else None)
            pending.append((bits, oa, flip(ob, CORE)))
            dgs.append(dg)
            gb1s.append(gb1)
            gb2s.append(gb2)
            nts.append(nt)
            saved.append(keep)

        unmix = split_mat.T
        nt_all = jnp.stack(nts)
        b, oa_p, th_p = pending.pop(0)
        mine = second_hop(b, oa_p, th_p)
        mine, nt_a = lax.optimization_barrier((mine, nt_all))
        outs.append(flip(mine, b))

        rel = [CHIPS[k // 2] ^ (CORE * (k % 2)) for k in range(n_dev)]
        dg_rel = jnp.stack([dg[:, k, :] for dg in dgs for k in range(2)])
        slot_of = jnp.array([rel.index(m) for m in range(n_dev)], jnp.int32)
        dg_abs = dg_rel[slot_of[jnp.arange(n_dev) ^ me]]
        dg_back = lax.all_to_all(dg_abs, ('ep', 'tp'), 0, 0, tiled=True)

        part_e = n_e // 2
        gw1_a, gw2_a = run_wgrad(nt_a, saved, unmix, 0, part_e)
        b, oa_p, th_p = pending.pop(0)
        mine = second_hop(b, oa_p, th_p)
        d_gate = jnp.sum(dg_back.reshape(ep_count, tp_count, n_e, toks), axis=1).reshape(n_experts, toks).T
        d_logits = w_full * (d_gate - jnp.sum(w_full * d_gate, axis=1, keepdims=True))
        mine, d_logits, nt_b, _ = lax.optimization_barrier((mine, d_logits, nt_all, gw2_a[0, 0, 0]))
        outs.append(flip(mine, b))
        gw1_b, gw2_b = run_wgrad(nt_b, saved, unmix, part_e, n_e - part_e)
        gw1 = jnp.concatenate([gw1_a, gw1_b])
        gw2 = jnp.concatenate([gw2_a, gw2_b])
        gb1 = functools.reduce(jnp.add, gb1s)[:, 0, :]
        gb1 = jnp.stack([gb1[:, :half], gb1[:, half:]], axis=2).reshape(n_e, wide)
        gb2 = functools.reduce(jnp.add, gb2s)[:, 0, :]

        d_all = lax.all_gather(d_logits, ('ep', 'tp'))
        d_all_b = d_all.astype(BF)
        gwr = 0.0
        for k, (_, xa, xb) in enumerate(pairs):
            for i, rows in enumerate((xa, xb)):
                gwr = gwr + jnp.einsum('td,te->de', rows[:toks], d_all_b[me ^ rel[2 * k + i]], preferred_element_type=F32)
        gbr = jnp.sum(d_all, axis=(0, 1))
        total = functools.reduce(jnp.add, [o.astype(F32) for o in outs])
        d_x = total[toks:] + jnp.einsum('te,de->td', d_logits.astype(BF), w_router, preferred_element_type=F32)
        return (total[:toks].astype(BF), d_x.astype(BF), gw1, gb1, gw2, gb2, gwr, gbr)

    in_specs = (tok_spec, tok_spec, tok_spec, P(None, None), P(None), P('ep', None, 'tp'), P('ep', 'tp'), P('ep', 'tp', None), P('ep', None), tok_spec)
    out_specs = (tok_spec, tok_spec, P('ep', None, 'tp'), P('ep', 'tp'), P('ep', 'tp', None), P('ep', None), P(None, None), P(None))
    return jax.shard_map(device_fn, mesh=mesh, in_specs=in_specs, out_specs=out_specs, check_vma=False)
```

time: 2920 us -> 419 us (0.14)
  waiting for transfers between devices: 2070 us -> 44.3 us
  matrix products: 364 us -> 14.8 us
  local copies, waits for them, and re-layouts: 256 us -> 12.2 us
  Pallas kernels: 0 us -> 219 us
  other arithmetic: 116 us -> 52 us
  starting transfers between devices: 65.4 us -> 20 us
    all_to_all x6 -> x1, waiting for transfers between devices: 1410 us -> 0.01 us  [device_fn(): dg_back = lax.all_to_all(dg_abs, ('ep', 'tp'), 0, 0, tiled=True)]
    all_gather x2 -> x0, waiting for transfers between devices: 667 us -> none  [dispatch(): lax.all_gather(buf_in.reshape(n_experts, capacity, model_dim), 'tp', axis=0)]
    dot_general x13 -> x11, matrix products: 364 us -> 14.8 us  [the longest x8 11.5 us: device_fn(): jnp.einsum('td,te->de', rows[:toks], d_all_b[me ^ rel[2 * k + i]], prefer...]
    pallas_call x0 -> x6, Pallas kernels: none -> 219 us  [the longest x4 179 us: run_chunk(): pl.pallas_call(functools.partial(chunk_kernel, first, toks), grid_spec=pl...]
    reduce_sum x7 -> x4, other arithmetic: 66.3 us -> 1.48 us  [the longest x1 0.78 us: device_fn(): w_full = jnp.sum(jnp.where(expert_hot, gate_w[:, :, None], 0.0), axis=1)]
    all_to_all x6 -> x1, starting transfers between devices: 65.2 us -> 7.48 us  [device_fn(): dg_back = lax.all_to_all(dg_abs, ('ep', 'tp'), 0, 0, tiled=True)]
    convert_element_type x3 -> x0, local copies, waits for them, and re-layouts: 56.5 us -> none  [the longest x1 22.7 us: device_fn(): jnp.einsum('sgecf,edf->sgecd', d_hidden_b, w_gate_up, preferred_element_t...]
    all_gather x0 -> x1, blocking collectives: none -> 50.7 us  [device_fn(): d_all = lax.all_gather(d_logits, ('ep', 'tp'))]
  transfers between devices with their start and end apart: 9 -> 15, of which waited for: 7 -> 2; matrix products, arithmetic and copies ran while one was open for 19% -> 12% of each run, Pallas kernels for 0% -> 53%
where the time goes in v2:
time: 419 us; the launch traced here: 414 us
  Pallas kernels  219 us (52%)
  other arithmetic  52 us (12%)
  blocking collectives  50.7 us (12%)
  waiting for transfers between devices  44.3 us (11%)
  starting transfers between devices  20 us (5%)
  matrix products  14.8 us (4%)
  local copies, waits for them, and re-layouts  12.2 us (3%)
    pallas_call x4, Pallas kernels, run_chunk(): pl.pallas_call(functools.partial(chunk_kernel, first, toks), grid_spec=pl...  179 us
    all_gather x1, blocking collectives, device_fn(): d_all = lax.all_gather(d_logits, ('ep', 'tp'))  50.7 us
    ppermute x14, waiting for transfers between devices, flip(): lax.ppermute(arr, ('tp', 'ep'), [(s, s ^ turned) for s in range(n_dev)])  44.3 us
    pallas_call x2, Pallas kernels, run_wgrad(): pl.pallas_call(functools.partial(wgrad_kernel, n_c, first_e), grid_spec=p...  39.8 us
    convert_element_type x3, other arithmetic, second_hop(): return mine.astype(BF) if bits else mine  13.5 us
    ppermute x14, starting transfers between devices, flip(): lax.ppermute(arr, ('tp', 'ep'), [(s, s ^ turned) for s in range(n_dev)])  12.5 us
    concatenate x1, other arithmetic, device_fn(): load = jnp.concatenate([x_loc, dy_loc, aux], axis=0)  11.9 us
    dot_general x8, matrix products, device_fn(): jnp.einsum('td,te->de', rows[:toks], d_all_b[me ^ rel[2 * k + i]], prefer...  11.5 us
  transfers between devices with their start and end apart: 15, of which 2 were waited for; matrix products, arithmetic and copies ran while one was open for 12% of the time, Pallas kernels for 53%

profile of v2, /device:TPU:0, one launch (start us, length us, event | category | flops | bytes accessed | tf_op | source)
XLA Modules:
  0.0 414.0 jit_solution(12228337408319750387)
XLA Ops:
  2.5 1.6 convolution_add_fusion.4
  6.5 11.9 %maximum_maximum_fusion.xa_ref = bf16[1088,1024]{1,0:T(8,128)(2,1)} fusion(bf16[32,512]{1,0:T(8,128)(2,1)S(1)} %fusion.4, bf16[32,512]{1,0:T(8,128)(2,1)S(1)} %get-tuple-element.143, bf16[32,512]{1,0:T(8,128)(2,1)S(1)} %get-tuple-element.144, bf16[32,512]{1,0:T(8,128)(2,1)S(1)} %get-tuple-element.142, bf16[512,1024]{1,0:T(8,128)(2,1)} %param.20, ...), kind=kLoop, calls=%fused_computation.9 | loop fusion | flops 13369344 | bytes 4456448 | tf_op jit(solution)/shard_map/concatenate | solution.py:354
  19.3 2.5 collective-permute-start.3
  27.8 48.3 %experts.4 = (bf16[1024,1024]{1,0:T(8,128)(2,1)}, bf16[1024,1024]{1,0:T(8,128)(2,1)}, f32[8,2,512]{2,1,0:T(2,128)}, f32[8,1,512]{2,1,0:T(1,128)}, f32[8,1,1024]{...) custom-call(s32[1]{0:T(128)} %bitcast.ep_ref, ...), custom_call_target="tpu_custom_call" | custom-call | flops 28000000000 | bytes 40000000 | tf_op jit(solution)/shard_map/experts/pallas_call | solution.py:216
  77.4 42.9 %collective-permute-done.6.xa_ref = bf16[1088,1024]{1,0:T(8,128)(2,1)} collective-permute-done((bf16[1088,1024]{1,0:T(8,128)(2,1)}, bf16[1088,1024]{1,0:T(8,128)(2,1)}, u32[]{:S(2)}, u32[]{:S(2)}) %collective-permute-start.6) | collective-permute-done | bytes 2228256 | tf_op jit(solution)/shard_map/ppermute | solution.py:328
  122.7 4.5 %convert_add_fusion.1 = f32[1024,1024]{1,0:T(8,128)} fusion(bf16[1024,1024]{1,0:T(8,128)(2,1)S(1)} %collective-permute-done.1, bf16[1024,1024]{1,0:T(8,128)(2,1)} %get-tuple-element.62), kind=kLoop, calls=%fused_computation.8 | loop fusion | flops 3145728 | bytes 8388608 | tf_op jit(solution)/shard_map/add | solution.py:372
  127.2 43.4 %experts.5 = (bf16[1024,1024]{1,0:T(8,128)(2,1)}, bf16[1024,1024]{1,0:T(8,128)(2,1)}, f32[8,2,512]{2,1,0:T(2,128)}, f32[8,1,512]{2,1,0:T(1,128)}, f32[8,1,1024]{...) custom-call(s32[1]{0:T(128)} %bitcast.ep_ref, ...), custom_call_target="tpu_custom_call" | custom-call | flops 28000000000 | bytes 40000000 | tf_op jit(solution)/shard_map/experts/pallas_call | solution.py:216
  171.0 43.4 %experts.6 = (bf16[1024,1024]{1,0:T(8,128)(2,1)}, bf16[1024,1024]{1,0:T(8,128)(2,1)}, f32[8,2,512]{2,1,0:T(2,128)}, f32[8,1,512]{2,1,0:T(1,128)}, f32[8,1,1024]{...) custom-call(s32[1]{0:T(128)} %bitcast.ep_ref, ...), custom_call_target="tpu_custom_call" | custom-call | flops 28000000000 | bytes 40000000 | tf_op jit(solution)/shard_map/experts/pallas_call | solution.py:216
  215.5 4.5 %add_convert_fusion.2 = bf16[1024,1024]{1,0:T(8,128)(2,1)} fusion(bf16[1024,1024]{1,0:T(8,128)(2,1)} %collective-permute-done.5, bf16[1024,1024]{1,0:T(8,128)(2,1)} %get-tuple-element.66), kind=kLoop, calls=%fused_computation.7 | loop fusion | flops 4194304 | bytes 6291456 | tf_op jit(solution)/shard_map/convert_element_type | solution.py:373
  220.0 43.6 %experts.7 = (bf16[1024,1024]{1,0:T(8,128)(2,1)}, bf16[1024,1024]{1,0:T(8,128)(2,1)}, f32[8,2,512]{2,1,0:T(2,128)}, f32[8,1,512]{2,1,0:T(1,128)}, f32[8,1,1024]{...) custom-call(s32[1]{0:T(128)} %bitcast.ep_ref, ...), custom_call_target="tpu_custom_call" | custom-call | flops 28000000000 | bytes 40000000 | tf_op jit(solution)/shard_map/experts/pallas_call | solution.py:216
  266.4 7.5 %all-to-all-start = ((f32[8,8,512]{2,1,0:T(8,128)}), f32[8,8,512]{2,1,0:T(8,128)S(1)}, u32[]{:S(2)}, u32[]{:S(2)}) async-start(f32[8,8,512]{2,1,0:T(8,128)} %gather_fusion.1), calls=%async_computation | async-start | bytes 262144 | tf_op jit(solution)/shard_map/all_to_all | solution.py:401
  275.2 4.6 %add_convert_fusion.1 = bf16[1024,1024]{1,0:T(8,128)(2,1)} fusion(bf16[1024,1024]{1,0:T(8,128)(2,1)} %collective-permute-done.9, bf16[1024,1024]{1,0:T(8,128)(2,1)} %get-tuple-element.70), kind=kLoop, calls=%fused_computation.6 | loop fusion | flops 4194304 | bytes 6291456 | tf_op jit(solution)/shard_map/convert_element_type | solution.py:373
  279.7 1.7 collective-permute-start.11
  283.9 18.6 %weight_grads.2 = (bf16[4,1024,512]{2,1,0:T(8,128)(2,1)}, bf16[4,256,1024]{2,1,0:T(8,128)(2,1)}) custom-call(s32[4,8]{1,0:T(4,128)} %pad_add_fusion.nt_ref, bf16[8,2,256,1024]{3,2,1,0:T(8,128)(2,1)} %get-tuple-element.87.refs_0_, bf16[8,2,256,1024]{3,2,1,0:T(8,128)(2,1)} %get-tuple-element.88.refs_1_, bf16[8,2,256,1024]{3,2,1,0:T(8,128)(2,1)} %get-tuple-element.89.refs_2_, ...), custom_call_target="tpu_custom_call" | custom-call | flops 25999998976 | bytes 60000000 | tf_op jit(solution)/shard_map/weight_grads/pallas_call | solution.py:299
  303.3 4.5 %add_convert_fusion = bf16[1024,1024]{1,0:T(8,128)(2,1)} fusion(bf16[1024,1024]{1,0:T(8,128)(2,1)} %collective-permute-done.12, bf16[1024,1024]{1,0:T(8,128)(2,1)} %get-tuple-element.78), kind=kLoop, calls=%fused_computation.5 | loop fusion | flops 4194304 | bytes 6291456 | tf_op jit(solution)/shard_map/convert_element_type | solution.py:373
  307.8 2.9 collective-permute-start.13
  310.6 21.2 %weight_grads.3 = (bf16[4,1024,512]{2,1,0:T(8,128)(2,1)}, bf16[4,256,1024]{2,1,0:T(8,128)(2,1)}) custom-call(s32[4,8]{1,0:T(4,128)} %pad_add_fusion.nt_ref, bf16[8,2,256,1024]{3,2,1,0:T(8,128)(2,1)} %get-tuple-element.87.refs_0_, bf16[8,2,256,1024]{3,2,1,0:T(8,128)(2,1)} %get-tuple-element.88.refs_1_, bf16[8,2,256,1024]{3,2,1,0:T(8,128)(2,1)} %get-tuple-element.89.refs_2_, ...), custom_call_target="tpu_custom_call" | custom-call | flops 25999998976 | bytes 60000000 | tf_op jit(solution)/shard_map/weight_grads/pallas_call | solution.py:299
  331.9 50.7 %all-gather = f32[4096,32]{0,1:T(8,128)S(1)} all-gather(f32[512,32]{0,1:T(8,128)S(1)} %fusion.21), channel_id=2, replica_groups=mesh['tp'=2,'ep'=4] {'ep','tp'}, dimensions={0}, use_global_device_ids=true | all-gather | bytes 589824 | tf_op jit(solution)/shard_map/all_gather | solution.py:418
  384.3 1.5 fusion.6
  385.8 2.4 pad_maximum_fusion.1
  391.2 1.5 fusion.1
  395.8 2.2 convolution_add_fusion
  398.0 7.6 %pad_maximum_fusion = bf16[8,1024,512]{2,1,0:T(8,128)(2,1)} fusion(bf16[4,1024,512]{2,1,0:T(8,128)(2,1)} %get-tuple-element.105, bf16[4,1024,512]{2,1,0:T(8,128)(2,1)} %get-tuple-element.103), kind=kLoop, calls=%fused_computation.2 | loop fusion | flops 4194304 | bytes 16777216 | tf_op jit(solution)/shard_map/concatenate | solution.py:412
  405.5 5.7 %convert_add_fusion = f32[1024,1024]{1,0:T(8,128)S(1)} fusion(bf16[1024,1024]{1,0:T(8,128)(2,1)} %collective-permute-done.13, bf16[1024,1024]{1,0:T(8,128)(2,1)} %collective-permute-done.11, f32[1024,1024]{1,0:T(8,128)} %convert_add_fusion.1, bf16[1024,1024]{1,0:T(8,128)(2,1)} %collective-permute-done.7), kind=kLoop, calls=%fused_computation.4 | loop fusion | flops 6291456 | bytes 14680064 | tf_op jit(solution)/shard_map/add | solution.py:425
  (122 shorter events, 33.5 us)
Async XLA Ops:
  18.4 7.9 %collective-permute-start = (bf16[1088,1024]{1,0:T(8,128)(2,1)}, bf16[1088,1024]{1,0:T(8,128)(2,1)S(1)}, u32[]{:S(2)}, u32[]{:S(2)}) collective-permute-start(bf16[1088,1024]{1,0:T(8,128)(2,1)} %maximum_maximum_fusion.xa_ref), channel_id=1, source_target_pairs={{0,1},{1,0},{2,3},{3,2},{4,5},{5,4},{6,7},{7,6}} | collective-permute-start | bytes 6684680 | tf_op jit(solution)/shard_map/ppermute | solution.py:328
  19.3 57.3 %collective-permute-start.3 = (bf16[1088,1024]{1,0:T(8,128)(2,1)}, bf16[1088,1024]{1,0:T(8,128)(2,1)}, u32[]{:S(2)}, u32[]{:S(2)}) collective-permute-start(bf16[1088,1024]{1,0:T(8,128)(2,1)} %maximum_maximum_fusion.xa_ref), channel_id=1, source_target_pairs={{0,2},{1,3},{2,0},{3,1},{4,6},{5,7},{6,4},{7,5}} | collective-permute-start | bytes 6684680 | tf_op jit(solution)/shard_map/ppermute | solution.py:328
  21.8 98.5 %collective-permute-start.6 = (bf16[1088,1024]{1,0:T(8,128)(2,1)}, bf16[1088,1024]{1,0:T(8,128)(2,1)}, u32[]{:S(2)}, u32[]{:S(2)}) collective-permute-start(bf16[1088,1024]{1,0:T(8,128)(2,1)} %maximum_maximum_fusion.xa_ref), channel_id=1, source_target_pairs={{0,6},{1,7},{2,4},{3,5},{4,2},{5,3},{6,0},{7,1}} | collective-permute-start | bytes 6684680 | tf_op jit(solution)/shard_map/ppermute | solution.py:328
  23.3 98.4 %collective-permute-start.2 = (bf16[1088,1024]{1,0:T(8,128)(2,1)}, bf16[1088,1024]{1,0:T(8,128)(2,1)}, u32[]{:S(2)}, u32[]{:S(2)}) collective-permute-start(bf16[1088,1024]{1,0:T(8,128)(2,1)} %maximum_maximum_fusion.xa_ref), channel_id=1, source_target_pairs={{0,5},{1,4},{2,7},{3,6},{4,1},{5,0},{6,3},{7,2}} | collective-permute-start | bytes 6684680 | tf_op jit(solution)/shard_map/ppermute | solution.py:328
  27.8 48.8 %copy-start.1 = (s32[8]{0:T(128)S(1)}, s32[8]{0:T(128)}, u32[]{:S(2)}) copy-start(s32[8]{0:T(128)} %constant.18.clone) | copy-start | bytes 100
  76.1 46.6 %collective-permute-start.1 = (bf16[1024,1024]{1,0:T(8,128)(2,1)}, bf16[1024,1024]{1,0:T(8,128)(2,1)S(1)}, u32[]{:S(2)}, u32[]{:S(2)}) collective-permute-start(bf16[1024,1024]{1,0:T(8,128)(2,1)} %get-tuple-element.63), channel_id=1, source_target_pairs={{0,1},{1,0},{2,3},{3,2},{4,5},{5,4},{6,7},{7,6}} | collective-permute-start | bytes 6291464 | tf_op jit(solution)/shard_map/ppermute | solution.py:328
  76.6 50.6 %collective-permute-start.4 = (bf16[1088,1024]{1,0:T(8,128)(2,1)}, bf16[1088,1024]{1,0:T(8,128)(2,1)}, u32[]{:S(2)}, u32[]{:S(2)}) collective-permute-start(bf16[1088,1024]{1,0:T(8,128)(2,1)} %collective-permute-done.3.xa_ref), channel_id=1, source_target_pairs={{0,1},{1,0},{2,3},{3,2},{4,5},{5,4},{6,7},{7,6}} | collective-permute-start | bytes 6684680 | tf_op jit(solution)/shard_map/ppermute | solution.py:328
  120.3 99.8 %collective-permute-start.10 = (bf16[1088,1024]{1,0:T(8,128)(2,1)}, bf16[1088,1024]{1,0:T(8,128)(2,1)}, u32[]{:S(2)}, u32[]{:S(2)}) collective-permute-start(bf16[1088,1024]{1,0:T(8,128)(2,1)} %collective-permute-done.6.xa_ref), channel_id=1, source_target_pairs={{0,1},{1,0},{2,3},{3,2},{4,5},{5,4},{6,7},{7,6}} | collective-permute-start | bytes 6684680 | tf_op jit(solution)/shard_map/ppermute | solution.py:328
  121.6 49.3 %collective-permute-start.8 = (bf16[1088,1024]{1,0:T(8,128)(2,1)}, bf16[1088,1024]{1,0:T(8,128)(2,1)}, u32[]{:S(2)}, u32[]{:S(2)}) collective-permute-start(bf16[1088,1024]{1,0:T(8,128)(2,1)} %collective-permute-done.2.xa_ref), channel_id=1, source_target_pairs={{0,1},{1,0},{2,3},{3,2},{4,5},{5,4},{6,7},{7,6}} | collective-permute-start | bytes 6684680 | tf_op jit(solution)/shard_map/ppermute | solution.py:328
  170.6 44.0 %copy-start.14 = (f32[8,2,512]{2,1,0:T(2,128)S(1)}, f32[8,2,512]{2,1,0:T(2,128)}, u32[]{:S(2)}) copy-start(f32[8,2,512]{2,1,0:T(2,128)} %get-tuple-element.81) | copy-start | bytes 98308
  170.7 44.9 %collective-permute-start.5 = (bf16[1024,1024]{1,0:T(8,128)(2,1)}, bf16[1024,1024]{1,0:T(8,128)(2,1)}, u32[]{:S(2)}, u32[]{:S(2)}) collective-permute-start(bf16[1024,1024]{1,0:T(8,128)(2,1)} %get-tuple-element.67), channel_id=1, source_target_pairs={{0,1},{1,0},{2,3},{3,2},{4,5},{5,4},{6,7},{7,6}} | collective-permute-start | bytes 6291464 | tf_op jit(solution)/shard_map/ppermute | solution.py:328
  214.4 60.8 %collective-permute-start.9 = (bf16[1024,1024]{1,0:T(8,128)(2,1)}, bf16[1024,1024]{1,0:T(8,128)(2,1)}, u32[]{:S(2)}, u32[]{:S(2)}) collective-permute-start(bf16[1024,1024]{1,0:T(8,128)(2,1)} %get-tuple-element.71), channel_id=1, source_target_pairs={{0,1},{1,0},{2,3},{3,2},{4,5},{5,4},{6,7},{7,6}} | collective-permute-start | bytes 6291464 | tf_op jit(solution)/shard_map/ppermute | solution.py:328
  220.0 53.8 %copy-start.20 = (s32[8]{0:T(128)S(1)}, s32[8]{0:T(128)}, u32[]{:S(2)}) copy-start(s32[8]{0:T(128)} %get-tuple-element.72) | copy-start | bytes 100
  220.0 53.8 %copy-start.21 = (s32[8]{0:T(128)S(1)}, s32[8]{0:T(128)}, u32[]{:S(2)}) copy-start(s32[8]{0:T(128)} %get-tuple-element.73) | copy-start | bytes 100
  220.0 53.8 %copy-start.22 = (s32[8]{0:T(128)S(1)}, s32[8]{0:T(128)}, u32[]{:S(2)}) copy-start(s32[8]{0:T(128)} %get-tuple-element.74) | copy-start | bytes 100
  263.7 39.6 %collective-permute-start.12 = (bf16[1024,1024]{1,0:T(8,128)(2,1)}, bf16[1024,1024]{1,0:T(8,128)(2,1)}, u32[]{:S(2)}, u32[]{:S(2)}) collective-permute-start(bf16[1024,1024]{1,0:T(8,128)(2,1)} %get-tuple-element.79), channel_id=1, source_target_pairs={{0,1},{1,0},{2,3},{3,2},{4,5},{5,4},{6,7},{7,6}} | collective-permute-start | bytes 6291464 | tf_op jit(solution)/shard_map/ppermute | solution.py:328
  266.4 36.8 %all-to-all-start = ((f32[8,8,512]{2,1,0:T(8,128)}), f32[8,8,512]{2,1,0:T(8,128)S(1)}, u32[]{:S(2)}, u32[]{:S(2)}) async-start(f32[8,8,512]{2,1,0:T(8,128)} %gather_fusion.1), calls=%async_computation | async-start | bytes 262144 | tf_op jit(solution)/shard_map/all_to_all | solution.py:401
  279.7 125.8 %collective-permute-start.11 = (bf16[1024,1024]{1,0:T(8,128)(2,1)}, bf16[1024,1024]{1,0:T(8,128)(2,1)}, u32[]{:S(2)}, u32[]{:S(2)}) collective-permute-start(bf16[1024,1024]{1,0:T(8,128)(2,1)} %add_convert_fusion.1), channel_id=1, source_target_pairs={{0,5},{1,4},{2,7},{3,6},{4,1},{5,0},{6,3},{7,2}} | collective-permute-start | bytes 6291464 | tf_op jit(solution)/shard_map/ppermute | solution.py:328
  281.5 124.1 %collective-permute-start.7 = (bf16[1024,1024]{1,0:T(8,128)(2,1)}, bf16[1024,1024]{1,0:T(8,128)(2,1)}, u32[]{:S(2)}, u32[]{:S(2)}) collective-permute-start(bf16[1024,1024]{1,0:T(8,128)(2,1)} %add_convert_fusion.2), channel_id=1, source_target_pairs={{0,2},{1,3},{2,0},{3,1},{4,6},{5,7},{6,4},{7,5}} | collective-permute-start | bytes 6291464 | tf_op jit(solution)/shard_map/ppermute | solution.py:328
  283.9 18.7 %copy-start.11 = (f32[8,1,1024]{2,1,0:T(1,128)S(1)}, f32[8,1,1024]{2,1,0:T(1,128)}, u32[]{:S(2)}) copy-start(f32[8,1,1024]{2,1,0:T(1,128)} %get-tuple-element.114) | copy-start | bytes 98308
  283.9 18.7 %copy-start.12 = (f32[8,1,1024]{2,1,0:T(1,128)S(1)}, f32[8,1,1024]{2,1,0:T(1,128)}, u32[]{:S(2)}) copy-start(f32[8,1,1024]{2,1,0:T(1,128)} %get-tuple-element.115) | copy-start | bytes 98308
  283.9 19.3 %copy-start.7 = (f32[512,32]{0,1:T(8,128)S(1)}, f32[512,32]{0,1:T(8,128)}, u32[]{:S(2)}) copy-start(f32[512,32]{0,1:T(8,128)} %copy-done.6) | copy-start | bytes 196612
  307.8 97.8 %collective-permute-start.13 = (bf16[1024,1024]{1,0:T(8,128)(2,1)}, bf16[1024,1024]{1,0:T(8,128)(2,1)}, u32[]{:S(2)}, u32[]{:S(2)}) collective-permute-start(bf16[1024,1024]{1,0:T(8,128)(2,1)} %add_convert_fusion), channel_id=1, source_target_pairs={{0,6},{1,7},{2,4},{3,5},{4,2},{5,3},{6,0},{7,1}} | collective-permute-start | bytes 6291464 | tf_op jit(solution)/shard_map/ppermute | solution.py:328
  331.8 52.1 %copy-start.3 = (bf16[512,1024]{1,0:T(8,128)(2,1)S(1)}, bf16[512,1024]{1,0:T(8,128)(2,1)}, u32[]{:S(2)}) copy-start(bf16[512,1024]{1,0:T(8,128)(2,1)} %param.11) | copy-start | bytes 3145732
  (14 other events, 119.6 us)
